TPU v7x, 32 devices: a whole 2x2x4 slice. The times are simulated.
32 devices in a mesh: dp: 8 (over y, x, core), tensor: 4 (over z).
Axes of the slice: x: 2, y: 2, z: 4, core: 2. Of those that a mesh axis runs over, the one named last changes fastest.
Arguments:
- tokens: bfloat16 [16384, 1024], P(('dp', 'tensor')), may hold values from -6 to 6
- lengths: int32 [8], P('dp'), may hold values from 120 to 2048, as said below
- ln1_gain: float32 [1024], replicated, may hold values from 0.1 to 1.9
- ln1_bias: float32 [1024], replicated, may hold values from -3 to 3
- w_query: bfloat16 [1024, 1024], P(None, 'tensor'), may hold values from -0.25 to 0.25
- w_key: bfloat16 [1024, 1024], P(None, 'tensor'), may hold values from -0.25 to 0.25
- w_value: bfloat16 [1024, 1024], P(None, 'tensor'), may hold values from -0.1875 to 0.1875
- w_out: bfloat16 [1024, 1024], P('tensor'), may hold values from -0.75 to 0.75
- ln2_gain: float32 [1024], replicated, may hold values from 0.1 to 1.9
- ln2_bias: float32 [1024], replicated, may hold values from -3 to 3
- w_gate: bfloat16 [1024, 4096], P(None, 'tensor'), may hold values from -0.1875 to 0.1875
- w_up: bfloat16 [1024, 4096], P(None, 'tensor'), may hold values from -0.1875 to 0.1875
- down_weight: bfloat16 [4096, 1024], P('tensor'), may hold values from -0.125 to 0.125
- cotangent: bfloat16 [16384, 1024], P(('dp', 'tensor')), may hold values from -6 to 6
Outputs:
- output: bfloat16 [16384, 1024], P(('dp', 'tensor'))
- input_grad: float32 [16384, 1024], P(('dp', 'tensor'))
- ln1_gain_grad: float32 [1024], replicated
- ln1_bias_grad: float32 [1024], replicated
- query_grad: float32 [1024, 1024], P(None, 'tensor')
- key_grad: float32 [1024, 1024], P(None, 'tensor')
- value_grad: float32 [1024, 1024], P(None, 'tensor')
- out_grad: float32 [1024, 1024], P('tensor')
- ln2_gain_grad: float32 [1024], replicated
- ln2_bias_grad: float32 [1024], replicated
- gate_grad: float32 [1024, 4096], P(None, 'tensor')
- up_grad: float32 [1024, 4096], P(None, 'tensor')
- down_grad: float32 [4096, 1024], P('tensor')
Inputs may be any that keep to these rules, and one draw needn't show every extreme that they name: `lengths`: real tokens of each window; every draw has a window of exactly 2048 and one of exactly 120.
All inputs are finite; a program needn't handle non-finite values.
Results may differ from a plain program's by a relative error of at most 0.023.
The roundings to bfloat16 on the way count: a program that leaves them out, or rounds other values in their place, can miss the bound.
Values may be sent and summed in bfloat16 or wider, within the bound.
A program may use at most 192 MiB of HBM per device.

v0:
```python
import math

import jax
import jax.numpy as jnp
from jax import lax
from jax.sharding import PartitionSpec as P

HD = 64


eps = 1e-05


def norm_parts(values, gain, shift):
    centre = jnp.mean(values, axis=-1, keepdims=True)
    centred = values - centre
    inverse = lax.rsqrt(jnp.mean(centred * centred, axis=-1, keepdims=True) + eps)
    scaled = centred * inverse
    return (scaled * gain + shift, scaled, inverse)


def norm_back(upstream, scaled, inverse, gain):
    through = upstream * gain
    inner = (
        through
        - jnp.mean(through, axis=-1, keepdims=True)
        - scaled * jnp.mean(through * scaled, axis=-1, keepdims=True)
    )
    return (inverse * inner, jnp.sum(upstream * scaled, axis=0), jnp.sum(upstream, axis=0))


def angle_tables(length, width):
    half_width = width // 2
    freqs = 10000.0 ** (-(jnp.arange(half_width, dtype=jnp.float32) * 2.0 / width))
    angles = jnp.arange(length, dtype=jnp.float32)[:, None] * freqs[None, :]
    return (jnp.cos(angles), jnp.sin(angles))


def rotate(values, cosine, sine):
    half_width = values.shape[-1] // 2
    first = values[..., :half_width]
    second = values[..., half_width:]
    return jnp.concatenate(
        [first * cosine - second * sine, second * cosine + first * sine], axis=-1
    )


def unrotate(values, cosine, sine):
    half_width = values.shape[-1] // 2
    first = values[..., :half_width]
    second = values[..., half_width:]
    return jnp.concatenate(
        [first * cosine + second * sine, second * cosine - first * sine], axis=-1
    )


def scores_block(query_block, key_rows, limit, factor):
    raw = (
        jnp.einsum("qhe,khe->hqk", query_block, key_rows, preferred_element_type=jnp.float32)
        * factor
    )
    live = lax.iota(jnp.int32, key_rows.shape[0]) < limit
    return jnp.where(live[None, None, :], raw, -1e30)


def attend(query, keys, values, lengths, block):
    windows, length, heads, depth = query.shape
    per_window = length // block
    factor = 1.0 / math.sqrt(depth)

    def one_block(index):
        window = index // per_window
        start = index % per_window * block
        query_win = lax.dynamic_index_in_dim(query, window, 0, keepdims=False)
        query_block = lax.dynamic_slice_in_dim(query_win, start, block, 0)
        key_rows = lax.dynamic_index_in_dim(keys, window, 0, keepdims=False)
        value_rows = lax.dynamic_index_in_dim(values, window, 0, keepdims=False)
        limit = lax.dynamic_index_in_dim(lengths, window, 0, keepdims=False)
        scores = scores_block(query_block, key_rows, limit, factor)
        peak = jnp.max(scores, axis=-1, keepdims=True)
        expos = jnp.exp(scores - peak)
        total = jnp.sum(expos, axis=-1, keepdims=True)
        probs_low = (expos / total).astype(jnp.bfloat16)
        context = jnp.einsum(
            "hqk,khe->qhe", probs_low, value_rows, preferred_element_type=jnp.float32
        ).astype(jnp.bfloat16)
        return (context, (peak + jnp.log(total))[..., 0])

    context, logsum = lax.map(one_block, jnp.arange(windows * per_window))
    return (context.reshape(query.shape), logsum.reshape(windows, per_window, heads, block))


def attend_back(query, keys, values, grad_context, logsum, lengths, block):
    windows, length, heads, depth = query.shape
    per_window = length // block
    factor = 1.0 / math.sqrt(depth)

    def one_window(window):
        query_win = lax.dynamic_index_in_dim(query, window, 0, keepdims=False)
        key_rows = lax.dynamic_index_in_dim(keys, window, 0, keepdims=False)
        value_rows = lax.dynamic_index_in_dim(values, window, 0, keepdims=False)
        grad_win = lax.dynamic_index_in_dim(grad_context, window, 0, keepdims=False)
        logsum_win = lax.dynamic_index_in_dim(logsum, window, 0, keepdims=False)
        limit = lax.dynamic_index_in_dim(lengths, window, 0, keepdims=False)

        def one_step(carry, step):
            key_grad, value_grad = carry
            start = step * block
            query_block = lax.dynamic_slice_in_dim(query_win, start, block, 0)
            grad_block = lax.dynamic_slice_in_dim(grad_win, start, block, 0)
            scores = scores_block(query_block, key_rows, limit, factor)
            level = lax.dynamic_index_in_dim(logsum_win, step, 0, keepdims=False)
            probs = jnp.exp(scores - level[:, :, None])
            probs_low = probs.astype(jnp.bfloat16)
            context = jnp.einsum(
                "hqk,khe->qhe", probs_low, value_rows, preferred_element_type=jnp.float32
            ).astype(jnp.bfloat16)
            grad_probs = jnp.einsum(
                "qhe,khe->hqk", grad_block, value_rows, preferred_element_type=jnp.float32
            )
            inner = jnp.sum(probs * grad_probs, axis=-1, keepdims=True)
            grad_scores = (probs * (grad_probs - inner)).astype(jnp.bfloat16)
            query_grad = (
                jnp.einsum(
                    "hqk,khe->qhe", grad_scores, key_rows, preferred_element_type=jnp.float32
                )
                * factor
            )
            key_grad = (
                key_grad
                + jnp.einsum(
                    "hqk,qhe->khe", grad_scores, query_block, preferred_element_type=jnp.float32
                )
                * factor
            )
            value_grad = value_grad + jnp.einsum(
                "hqk,qhe->khe", probs_low, grad_block, preferred_element_type=jnp.float32
            )
            return ((key_grad, value_grad), (query_grad, context))

        zero_rows = jnp.zeros(key_rows.shape, jnp.float32)
        (key_grad, value_grad), (query_grad, context) = lax.scan(
            one_step, (zero_rows, zero_rows), jnp.arange(per_window)
        )
        return (
            query_grad.reshape(key_rows.shape),
            key_grad,
            value_grad,
            context.reshape(key_rows.shape),
        )

    return lax.map(one_window, jnp.arange(windows))


def on_device(
    tokens,
    lengths,
    ln1_gain,
    ln1_bias,
    w_query,
    w_key,
    w_value,
    w_out,
    ln2_gain,
    ln2_bias,
    w_gate,
    w_up,
    down_weight,
    cotangent,
):
    local_rows = tokens.shape[0]
    group_rows = local_rows * lax.axis_size("tensor")
    windows = lengths.shape[0]
    length = group_rows // windows
    block = min(512, length)
    heads_here = w_query.shape[1] // HD
    width_here = heads_here * HD
    hidden_here = w_gate.shape[1]
    row_ids = lax.axis_index("tensor") * local_rows + lax.iota(jnp.int32, local_rows)
    window_ids = row_ids // length
    limits = jnp.sum(
        jnp.where(
            window_ids[:, None] == lax.iota(jnp.int32, windows)[None, :], lengths[None, :], 0
        ),
        axis=1,
    )
    valid = (row_ids % length < limits)[:, None]
    cosine, sine = angle_tables(length, HD)
    cosine = cosine[None, :, None, :]
    sine = sine[None, :, None, :]
    w_qkv = jnp.concatenate([w_query, w_key, w_value], axis=1)
    w_pair = jnp.concatenate([w_gate, w_up], axis=1)

    def project(rows_full):
        mixed = jnp.dot(rows_full, w_qkv, preferred_element_type=jnp.float32)
        shaped = mixed.reshape(windows, length, 3, heads_here, HD)
        query = rotate(shaped[:, :, 0], cosine, sine).astype(jnp.bfloat16)
        keys = rotate(shaped[:, :, 1], cosine, sine).astype(jnp.bfloat16)
        values = shaped[:, :, 2].astype(jnp.bfloat16)
        return (query, keys, values)

    def gated(rows_full):
        both = jnp.dot(rows_full, w_pair, preferred_element_type=jnp.float32)
        gate = both[:, :hidden_here]
        upper = both[:, hidden_here:]
        sigma = jax.nn.sigmoid(gate)
        return (gate, upper, sigma, (gate * sigma * upper).astype(jnp.bfloat16))

    inputs = tokens.astype(jnp.float32)
    normed1, scaled1, inverse1 = norm_parts(inputs, ln1_gain, ln1_bias)
    attn_in = normed1.astype(jnp.bfloat16)
    attn_rows = lax.all_gather(attn_in, "tensor", axis=0, tiled=True)
    query, keys, values = project(attn_rows)
    context, logsum = attend(query, keys, values, lengths, block)
    context_rows = context.reshape(group_rows, width_here)
    picked = context_rows
    attn_out = lax.psum_scatter(
        jnp.dot(picked, w_out, preferred_element_type=jnp.float32)
        .astype(jnp.bfloat16)
        .astype(jnp.float32)
        .astype(jnp.bfloat16),
        "tensor",
        scatter_dimension=0,
        tiled=True,
    ).astype(jnp.float32)
    middle = inputs + attn_out
    normed2, scaled2, inverse2 = norm_parts(middle, ln2_gain, ln2_bias)
    ffn_in = normed2.astype(jnp.bfloat16)
    ffn_rows = lax.all_gather(ffn_in, "tensor", axis=0, tiled=True)
    hidden_activations = gated(ffn_rows)[3]
    picked = hidden_activations
    ffn_out = lax.psum_scatter(
        jnp.dot(picked, down_weight, preferred_element_type=jnp.float32)
        .astype(jnp.bfloat16)
        .astype(jnp.float32)
        .astype(jnp.bfloat16),
        "tensor",
        scatter_dimension=0,
        tiled=True,
    ).astype(jnp.float32)
    output = jnp.where(valid, middle + ffn_out, 0.0).astype(jnp.bfloat16)
    grad_out = jnp.where(valid, cotangent.astype(jnp.float32), 0.0)
    grad_branch = lax.all_gather(grad_out.astype(jnp.bfloat16), "tensor", axis=0, tiled=True)
    ffn_back = lax.all_gather(ffn_in, "tensor", axis=0, tiled=True)
    gate, upper, sigma, hidden_back = gated(ffn_back)
    down_grad = jnp.einsum(
        "rf,rd->fd", hidden_back, grad_branch, preferred_element_type=jnp.float32
    )
    grad_hidden = jnp.einsum(
        "rd,fd->rf", grad_branch, down_weight, preferred_element_type=jnp.float32
    )
    grad_gate = grad_hidden * upper * sigma * (1.0 + gate * (1.0 - sigma))
    grad_upper = grad_hidden * gate * sigma
    grad_pair = jnp.concatenate([grad_gate, grad_upper], axis=1).astype(jnp.bfloat16)
    pair_grad = jnp.einsum("rd,rf->df", ffn_back, grad_pair, preferred_element_type=jnp.float32)
    gate_grad = pair_grad[:, :hidden_here]
    up_grad = pair_grad[:, hidden_here:]
    picked = grad_pair
    grad_ffn_in = lax.psum_scatter(
        jnp.einsum("rf,df->rd", picked, w_pair, preferred_element_type=jnp.float32)
        .astype(jnp.bfloat16)
        .astype(jnp.float32)
        .astype(jnp.bfloat16),
        "tensor",
        scatter_dimension=0,
        tiled=True,
    ).astype(jnp.float32)
    grad_norm2, gain2_grad, shift2_grad = norm_back(grad_ffn_in, scaled2, inverse2, ln2_gain)
    grad_middle = grad_out + grad_norm2
    grad_attn = lax.all_gather(grad_middle.astype(jnp.bfloat16), "tensor", axis=0, tiled=True)
    attn_back = lax.all_gather(attn_in, "tensor", axis=0, tiled=True)
    query, keys, values = project(attn_back)
    grad_context = jnp.einsum(
        "rd,cd->rc", grad_attn, w_out, preferred_element_type=jnp.float32
    ).astype(jnp.bfloat16)
    grad_context = grad_context.reshape(windows, length, heads_here, HD)
    query_back, key_back, value_back, context_back = attend_back(
        query, keys, values, grad_context, logsum, lengths, block
    )
    out_grad = jnp.einsum(
        "rc,rd->cd",
        context_back.reshape(group_rows, width_here),
        grad_attn,
        preferred_element_type=jnp.float32,
    )
    grad_mixed = jnp.concatenate(
        [
            unrotate(query_back, cosine, sine).reshape(group_rows, width_here),
            unrotate(key_back, cosine, sine).reshape(group_rows, width_here),
            value_back.reshape(group_rows, width_here),
        ],
        axis=1,
    ).astype(jnp.bfloat16)
    qkv_grad = jnp.einsum("rd,rc->dc", attn_back, grad_mixed, preferred_element_type=jnp.float32)
    query_grad = qkv_grad[:, :width_here]
    key_grad = qkv_grad[:, width_here : 2 * width_here]
    value_grad = qkv_grad[:, 2 * width_here :]
    picked = grad_mixed
    grad_attn_in = lax.psum_scatter(
        jnp.einsum("rc,dc->rd", picked, w_qkv, preferred_element_type=jnp.float32)
        .astype(jnp.bfloat16)
        .astype(jnp.float32)
        .astype(jnp.bfloat16),
        "tensor",
        scatter_dimension=0,
        tiled=True,
    ).astype(jnp.float32)
    grad_norm1, gain1_grad, shift1_grad = norm_back(grad_attn_in, scaled1, inverse1, ln1_gain)
    input_grad = grad_middle + grad_norm1
    query_grad, key_grad, value_grad, out_grad, gate_grad, up_grad, down_grad = (
        lax.psum(query_grad.astype(jnp.bfloat16), "dp").astype(jnp.float32),
        lax.psum(key_grad.astype(jnp.bfloat16), "dp").astype(jnp.float32),
        lax.psum(value_grad.astype(jnp.bfloat16), "dp").astype(jnp.float32),
        lax.psum(out_grad.astype(jnp.bfloat16), "dp").astype(jnp.float32),
        lax.psum(gate_grad.astype(jnp.bfloat16), "dp").astype(jnp.float32),
        lax.psum(up_grad.astype(jnp.bfloat16), "dp").astype(jnp.float32),
        lax.psum(down_grad.astype(jnp.bfloat16), "dp").astype(jnp.float32),
    )
    gain1_grad, shift1_grad, gain2_grad, shift2_grad = lax.psum(
        (gain1_grad, shift1_grad, gain2_grad, shift2_grad), ("dp", "tensor")
    )
    return (
        output,
        input_grad,
        gain1_grad,
        shift1_grad,
        query_grad,
        key_grad,
        value_grad,
        out_grad,
        gain2_grad,
        shift2_grad,
        gate_grad,
        up_grad,
        down_grad,
    )


def solution(mesh):
    return jax.shard_map(
        on_device,
        mesh=mesh,
        in_specs=(
            P(("dp", "tensor"), None),
            P("dp"),
            P(),
            P(),
            P(None, "tensor"),
            P(None, "tensor"),
            P(None, "tensor"),
            P("tensor", None),
            P(),
            P(),
            P(None, "tensor"),
            P(None, "tensor"),
            P("tensor", None),
            P(("dp", "tensor"), None),
        ),
        out_specs=(
            P(("dp", "tensor"), None),
            P(("dp", "tensor"), None),
            P(),
            P(),
            P(None, "tensor"),
            P(None, "tensor"),
            P(None, "tensor"),
            P("tensor", None),
            P(),
            P(),
            P(None, "tensor"),
            P(None, "tensor"),
            P("tensor", None),
        ),
        check_vma=False,
    )
```

profile of v0, /device:TPU:9, one launch (start us, length us, event | category | flops | bytes accessed | tf_op | source)
XLA Modules:
  0.0 1283.9 jit_solution(5398323214661166941)
XLA Ops:
  18.6 74.8 %all-gather.5.cloned.1.call-done = bf16[2048,1024]{1,0:T(8,128)(2,1)} async-done(((bf16[512,1024]{1,0:T(8,128)(2,1)}), bf16[2048,1024]{1,0:T(8,128)(2,1)}) %all-gather.5.cloned.1.call-update) | async-done | bytes 4194320 | tf_op jit(solution)/shard_map/all_gather | solution.py:212
  93.3 5.8 fusion.82
  104.8 64.1 %while.44 = (s32[]{:T(128)}, bf16[4,512,4,64]{1,3,2,0:T(8,128)(2,1)}, f32[4,4,512]{2,1,0:T(4,128)S(1)}, s32[1]{0:T(128)}, s32[4]{0:T(128)S(1)}, /*index=5*/bf16[...) while((s32[]{:T(128)}, ...), condition=%wide.region_5.6_spmd, body=%wide.region_2.5_spmd.sunk | while | flops 1124204544 | bytes 57221472 | solution.py:89
  174.9 77.7 %reduce-scatter.5.cloned.1.call-done = bf16[512,1024]{1,0:T(8,128)(2,1)} async-done(((bf16[2048,1024]{1,0:T(8,128)(2,1)}), bf16[512,1024]{1,0:T(8,128)(2,1)}) %reduce-scatter.5.cloned.1.call-update) | async-done | bytes 1048592 | tf_op jit(solution)/shard_map/reduce_scatter | solution.py:217
  265.5 70.9 %all-gather.7.cloned.1.call-done = bf16[2048,1024]{1,0:T(8,128)(2,1)} async-done(((bf16[512,1024]{1,0:T(8,128)(2,1)}), bf16[2048,1024]{1,0:T(8,128)(2,1)}) %all-gather.7.cloned.1.call-update) | async-done | bytes 4194320 | tf_op jit(solution)/shard_map/all_gather | solution.py:229
  336.4 15.2 %fusion.83 = f32[2048,2048]{0,1:T(8,128)} fusion(bf16[2048,1024]{1,0:T(8,128)(2,1)} %all-gather.7.cloned.1.call-done, bf16[1024,2048]{1,0:T(8,128)(2,1)} %constant_dynamic-update-slice_fusion.3), kind=kOutput, calls=%fused_computation.160 | convolution fusion | flops 8589934592 | bytes 25165824 | tf_op jit(solution)/shard_map/dot_general | solution.py:203
  351.6 66.2 %all-gather.9.cloned.1.call-done = bf16[2048,1024]{1,0:T(8,128)(2,1)} async-done(((bf16[512,1024]{1,0:T(8,128)(2,1)}), bf16[2048,1024]{1,0:T(8,128)(2,1)}) %all-gather.9.cloned.1.call-update) | async-done | bytes 4194320 | tf_op jit(solution)/shard_map/all_gather | solution.py:243
  417.8 13.3 %multiply_convert_fusion.2 = (bf16[2048,1024]{0,1:T(8,128)(2,1)S(1)}, bf16[2048,1024]{0,1:T(8,128)(2,1)S(1)}, bf16[2048,1024]{0,1:T(8,128)(2,1)}) fusion(f32[2048,2048]{0,1:T(8,128)} %fusion.83, bf16[2048,1024]{1,0:T(8,128)(2,1)} %all-gather.9.cloned.1.call-done, bf16[1024,1024]{1,0:T(8,128)(2,1)S(1)} %copy-done), kind=kOutput, calls=%fused_computation.51 | convolution fusion | flops 4328521728 | bytes 35651584 | tf_op jit(solution)/shard_map/rd,fd->rf/dot_general | solution.py:249
  434.4 12.1 fusion.39
  446.6 17.7 %convolution_convert_fusion.3 = bf16[2048,1024]{1,0:T(8,128)(2,1)} fusion(bf16[2048,1024]{0,1:T(8,128)(2,1)} %get-tuple-element.326, bf16[1024,1024]{1,0:T(8,128)(2,1)S(1)} %copy-done), kind=kOutput, calls=%fused_computation.60 | convolution fusion | flops 4297064448 | bytes 10485760 | tf_op jit(solution)/shard_map/dot_general | solution.py:233
  464.4 60.2 %reduce-scatter.9.cloned.1.call-done = bf16[512,1024]{1,0:T(8,128)(2,1)} async-done(((bf16[2048,1024]{1,0:T(8,128)(2,1)}), bf16[512,1024]{1,0:T(8,128)(2,1)}) %reduce-scatter.9.cloned.1.call-update) | async-done | bytes 1048592 | tf_op jit(solution)/shard_map/reduce_scatter | solution.py:259
  527.5 77.0 %reduce-scatter.7.cloned.1.call-done = bf16[512,1024]{1,0:T(8,128)(2,1)} async-done(((bf16[2048,1024]{1,0:T(8,128)(2,1)}), bf16[512,1024]{1,0:T(8,128)(2,1)}) %reduce-scatter.7.cloned.1.call-update) | async-done | bytes 1048592 | tf_op jit(solution)/shard_map/reduce_scatter | solution.py:232
  611.6 11.5 fusion.40
  628.2 5.7 convolution_convert_fusion.5
  634.0 53.9 %all-gather.11.cloned.1.call-done = bf16[2048,1024]{1,0:T(8,128)(2,1)} async-done(((bf16[512,1024]{1,0:T(8,128)(2,1)}), bf16[2048,1024]{1,0:T(8,128)(2,1)}) %all-gather.11.cloned.1.call-update) | async-done | bytes 4194320 | tf_op jit(solution)/shard_map/all_gather | solution.py:270
  693.3 310.0 %while.45 = (s32[]{:T(128)}, f32[2048,4,64]{0,2,1:T(8,128)}, f32[2048,4,64]{0,2,1:T(8,128)}, f32[4,512,4,64]{1,0,3,2:T(4,128)}, bf16[4,512,4,64]{1,3,2,0:T(8,128...) while((s32[]{:T(128)}, f32[2048,4,64]{0,2,1:T(8,128)}, ...), condition=%wide.region_15.16_spmd.clone, body=%wide.region_13.15_spmd.clone.sunk | while | flops 3303800832 | bytes 259860816 | solution.py:142
  697.6 9.1 fusion.145
  706.7 10.1 fusion.149
  716.8 11.0 fusion.147
  727.8 9.9 multiply_reduce_fusion.3
  737.7 10.7 multiply_convert_fusion.5
  748.4 6.2 fusion.148
  759.0 11.1 dynamic_update_slice.43
  774.0 9.1 fusion.145
  783.0 10.1 fusion.149
  793.1 11.6 fusion.147
  804.7 9.9 multiply_reduce_fusion.3
  814.6 10.7 multiply_convert_fusion.5
  825.3 6.2 fusion.148
  836.7 11.1 dynamic_update_slice.43
  851.6 9.1 fusion.145
  860.7 10.1 fusion.149
  870.8 11.6 fusion.147
  882.4 9.9 multiply_reduce_fusion.3
  892.3 10.7 multiply_convert_fusion.5
  903.0 6.2 fusion.148
  914.4 11.1 dynamic_update_slice.43
  929.3 9.1 fusion.145
  938.4 10.1 fusion.149
  948.5 11.6 fusion.147
  960.1 9.9 multiply_reduce_fusion.3
  970.0 10.7 multiply_convert_fusion.5
  980.7 6.2 fusion.148
  992.1 11.1 dynamic_update_slice.43
  1023.1 6.7 convolution_convert_fusion.2
  1029.8 121.4 %all-reduce.4.cloned.1.call-done = (bf16[1024,256]{1,0:T(8,128)(2,1)}, bf16[1024,256]{1,0:T(8,128)(2,1)}, bf16[1024,256]{1,0:T(8,128)(2,1)}, bf16[256,1024]{1,0:...) async-done(((bf16[1024,256]{1,0:T(8,128)(2,1)}, bf16[1024,256]{1,0:T(8,128)(2,1)}, bf16[1024,256]{1,0:T(8,128)(2,1)}, ...) | async-done | bytes 8388624 | tf_op jit(solution)/shard_map/psum | solution.py:311
  1166.3 64.9 %reduce-scatter.11.cloned.1.call-done = bf16[512,1024]{1,0:T(8,128)(2,1)} async-done(((bf16[2048,1024]{1,0:T(8,128)(2,1)}), bf16[512,1024]{1,0:T(8,128)(2,1)}) %reduce-scatter.11.cloned.1.call-update) | async-done | bytes 1048592 | tf_op jit(solution)/shard_map/reduce_scatter | solution.py:299
  1233.5 39.8 %all-reduce = (f32[1024]{0:T(1024)}, f32[1024]{0:T(1024)}, f32[1024]{0:T(1024)}, f32[1024]{0:T(1024)}) all-reduce(f32[1024]{0:T(1024)S(1)} %get-tuple-element.261, f32[1024]{0:T(1024)S(1)} %get-tuple-element.266, f32[1024]{0:T(1024)S(1)} %copy-done.41, f32[1024]{0:T(1024)S(1)} %copy-done.42), channel_id=1, replica_groups=mesh['dp'=8,'tensor'=4] {'dp','tensor'}, use_global_device_ids=true, to_apply=%region_20.21 | all-reduce | flops 4096 | bytes 32768 | tf_op jit(solution)/shard_map/psum | solution.py:319
  (244 shorter events, 181.0 us)
Async XLA Ops:
  7.2 410.7 %copy-start = (bf16[1024,1024]{1,0:T(8,128)(2,1)S(1)}, bf16[1024,1024]{1,0:T(8,128)(2,1)}, u32[]{:S(2)}) copy-start(bf16[1024,1024]{1,0:T(8,128)(2,1)} %param.30) | copy-start | bytes 6291460
  7.2 6.7 copy-start.33
  7.2 7.5 copy-start.34
  7.2 86.1 %all-gather.5.cloned.1.call-start = ((), (), s32[]{:S(2)}) async-start(), calls=%async_computation.4 | async-start | bytes 5242880 | tf_op jit(solution)/shard_map/all_gather | solution.py:212
  13.8 238.8 %reduce-scatter.5.cloned.1.call-start = ((), (), s32[]{:S(2)}) async-start(), calls=%async_computation.5 | async-start | bytes 5242880 | tf_op jit(solution)/shard_map/reduce_scatter | solution.py:217
  18.5 82.5 %copy-start.15 = (f32[2048,32]{0,1:T(8,128)}, f32[2048,32]{0,1:T(8,128)S(1)}, u32[]{:S(2)}) copy-start(f32[2048,32]{0,1:T(8,128)S(1)} %get-tuple-element.349) | copy-start | bytes 786436
  18.5 82.5 %copy-start.17 = (f32[2048,32]{0,1:T(8,128)}, f32[2048,32]{0,1:T(8,128)S(1)}, u32[]{:S(2)}) copy-start(f32[2048,32]{0,1:T(8,128)S(1)} %get-tuple-element.350) | copy-start | bytes 786436
  111.5 3.8 copy-start.24
  127.5 3.8 copy-start.24
  143.5 3.8 copy-start.24
  174.6 78.0 %copy-start.4 = (bf16[512,1024]{1,0:T(8,128)(2,1)S(1)}, bf16[512,1024]{1,0:T(8,128)(2,1)}, u32[]{:S(2)}) copy-start(bf16[512,1024]{1,0:T(8,128)(2,1)} %param.18) | copy-start | bytes 3145732
  174.6 81.4 %copy-start.37 = (f32[1024]{0:T(1024)S(1)}, f32[1024]{0:T(1024)}, u32[]{:S(2)}) copy-start(f32[1024]{0:T(1024)} %param.26) | copy-start | bytes 12292
  174.6 81.4 %copy-start.43 = (f32[1024]{0:T(1024)S(1)}, f32[1024]{0:T(1024)}, u32[]{:S(2)}) copy-start(f32[1024]{0:T(1024)} %param.27) | copy-start | bytes 12292
  174.6 161.8 %all-gather.7.cloned.1.call-start = ((), (), s32[]{:S(2)}) async-start(), calls=%async_computation.6 | async-start | bytes 5242880 | tf_op jit(solution)/shard_map/all_gather | solution.py:229
  257.6 160.3 %all-gather.9.cloned.1.call-start = ((), (), s32[]{:S(2)}) async-start(), calls=%async_computation.8 | async-start | bytes 5242880 | tf_op jit(solution)/shard_map/all_gather | solution.py:243
  260.8 263.8 %reduce-scatter.9.cloned.1.call-start = ((), (), s32[]{:S(2)}) async-start(), calls=%async_computation.9 | async-start | bytes 5242880 | tf_op jit(solution)/shard_map/reduce_scatter | solution.py:259
  446.5 158.0 %reduce-scatter.7.cloned.1.call-start = ((), (), s32[]{:S(2)}) async-start(), calls=%async_computation.7 | async-start | bytes 5242880 | tf_op jit(solution)/shard_map/reduce_scatter | solution.py:232
  464.3 60.3 %copy-start.8 = (bf16[512,1024]{1,0:T(8,128)(2,1)S(1)}, bf16[512,1024]{1,0:T(8,128)(2,1)}, u32[]{:S(2)}) copy-start(bf16[512,1024]{1,0:T(8,128)(2,1)} %reduce-scatter.5.cloned.1.call-done) | copy-start | bytes 3145732
  464.3 223.5 %all-gather.11.cloned.1.call-start = ((), (), s32[]{:S(2)}) async-start(), calls=%async_computation.10 | async-start | bytes 5242880 | tf_op jit(solution)/shard_map/all_gather | solution.py:270
  527.5 81.5 %copy-start.10 = (bf16[1,2048,4,32]{1,3,2,0:T(8,128)(2,1)S(1)}, bf16[1,2048,4,32]{1,3,2,0:T(8,128)(2,1)}, u32[]{:S(2)}) copy-start(bf16[1,2048,4,32]{1,3,2,0:T(8,128)(2,1)} %copy-done.9) | copy-start | bytes 1572868
  527.5 81.5 %copy-start.12 = (bf16[1,2048,4,32]{1,3,2,0:T(8,128)(2,1)S(1)}, bf16[1,2048,4,32]{1,3,2,0:T(8,128)(2,1)}, u32[]{:S(2)}) copy-start(bf16[1,2048,4,32]{1,3,2,0:T(8,128)(2,1)} %copy-done.11) | copy-start | bytes 1572868
  609.0 542.2 %all-reduce.4.cloned.1.call-start = ((), (), s32[]{:S(2)}) async-start(), calls=%async_computation.12 | async-start | bytes 16777216 | tf_op jit(solution)/shard_map/psum | solution.py:311
  623.2 5.0 copy-start.48
  628.2 59.6 %copy-start.31 = (bf16[256,1024]{1,0:T(8,128)(2,1)S(1)}, bf16[256,1024]{1,0:T(8,128)(2,1)}, u32[]{:S(2)}) copy-start(bf16[256,1024]{1,0:T(8,128)(2,1)} %param.25) | copy-start | bytes 1572868
  716.8 11.0 copy-start.2
  748.4 6.2 copy-start.3
  793.1 11.6 copy-start.2
  825.3 6.2 copy-start.3
  870.8 11.6 copy-start.2
  903.0 6.2 copy-start.3
  948.5 11.6 copy-start.2
  980.7 6.2 copy-start.3
  1006.8 4.8 copy-start.6
  1006.8 4.8 copy-start.16
  1006.8 4.8 copy-start.18
  1014.1 4.2 copy-start.27
  1014.7 4.7 copy-start.29
  1014.7 4.7 copy-start.45
  1021.6 209.6 %reduce-scatter.11.cloned.1.call-start = ((), (), s32[]{:S(2)}) async-start(), calls=%async_computation.11 | async-start | bytes 5242880 | tf_op jit(solution)/shard_map/reduce_scatter | solution.py:299
  1151.2 6.4 copy-start.32
  1151.2 7.5 copy-start.21
  1163.7 67.5 %copy-start.5 = (bf16[512,1024]{1,0:T(8,128)(2,1)S(1)}, bf16[512,1024]{1,0:T(8,128)(2,1)}, u32[]{:S(2)}) copy-start(bf16[512,1024]{1,0:T(8,128)(2,1)} %param.18) | copy-start | bytes 3145732
  1163.7 67.5 %copy-start.36 = (f32[512]{0:T(512)S(1)}, f32[512]{0:T(512)}, u32[]{:S(2)}) copy-start(f32[512]{0:T(512)} %copy-done.35) | copy-start | bytes 6148
  1163.7 67.5 %copy-start.38 = (f32[1024]{0:T(1024)S(1)}, f32[1024]{0:T(1024)}, u32[]{:S(2)}) copy-start(f32[1024]{0:T(1024)} %param.20) | copy-start | bytes 12292
  1163.7 67.5 %copy-start.40 = (f32[512]{0:T(512)S(1)}, f32[512]{0:T(512)}, u32[]{:S(2)}) copy-start(f32[512]{0:T(512)} %copy-done.39) | copy-start | bytes 6148
  1163.8 69.6 %copy-start.41 = (f32[1024]{0:T(1024)S(1)}, f32[1024]{0:T(1024)}, u32[]{:S(2)}) copy-start(f32[1024]{0:T(1024)} %get-tuple-element.259) | copy-start | bytes 12292
  1163.8 69.6 %copy-start.42 = (f32[1024]{0:T(1024)S(1)}, f32[1024]{0:T(1024)}, u32[]{:S(2)}) copy-start(f32[1024]{0:T(1024)} %get-tuple-element.265) | copy-start | bytes 12292
  1163.8 113.3 %copy-start.1 = (bf16[1024,1024]{1,0:T(8,128)(2,1)S(1)}, bf16[1024,1024]{1,0:T(8,128)(2,1)}, u32[]{:S(2)}) copy-start(bf16[1024,1024]{1,0:T(8,128)(2,1)} %param.30) | copy-start | bytes 6291460
  (21 other events, 51.6 us)
Sparse Core Ops, SparseCore 0:
  13.9 79.3 all-gather.4
  174.7 77.8 reduce-scatter.4
  257.7 78.6 all-gather.6
  338.5 79.2 all-gather.8
  446.7 77.8 reduce-scatter.8
  527.3 77.2 reduce-scatter.6
  609.1 78.6 all-gather.10
  1021.7 129.4 all-reduce.3
  1153.5 77.6 reduce-scatter.10
where the time goes:
time: 1300 us; the launch traced here: 1280 us
  waiting for transfers between devices  667 us (51%)
  matrix products  342 us (26%)
  other arithmetic  114 us (9%)
  local copies, waits for them, and re-layouts  86.3 us (7%)
  blocking collectives  39.8 us (3%)
  loops' own time  19 us (1%)
  between operations  15.2 us (1%)
    psum x1, waiting for transfers between devices, on_device(): lax.psum(query_grad.astype(jnp.bfloat16), 'dp').astype(jnp.float32)  121 us
    reduce_scatter x1, waiting for transfers between devices, on_device(): lax.psum_scatter(jnp.dot(picked, w_out, preferred_element_type=jnp.float3...  77.7 us
    reduce_scatter x1, waiting for transfers between devices, on_device(): lax.psum_scatter(jnp.dot(picked, down_weight, preferred_element_type=jnp....  77 us
    all_gather x1, waiting for transfers between devices, on_device(): attn_rows = lax.all_gather(attn_in, 'tensor', axis=0, tiled=True)  74.8 us
    all_gather x1, waiting for transfers between devices, on_device(): ffn_rows = lax.all_gather(ffn_in, 'tensor', axis=0, tiled=True)  70.9 us
    all_gather x1, waiting for transfers between devices, on_device(): lax.all_gather(grad_out.astype(jnp.bfloat16), 'tensor', axis=0, tiled=True)  66.2 us
    reduce_scatter x1, waiting for transfers between devices, on_device(): lax.psum_scatter(jnp.einsum('rc,dc->rd', picked, w_qkv, preferred_element...  64.9 us
    reduce_scatter x1, waiting for transfers between devices, on_device(): lax.psum_scatter(jnp.einsum('rf,df->rd', picked, w_pair, preferred_elemen...  60.2 us
  transfers between devices with their start and end apart: 9, of which 9 were waited for; matrix products, arithmetic and copies ran while one was open for 7% of the time, Pallas kernels for 0%

commit v1 on v0

v1 whole, which is shorter than its diff:
```python
import functools
import math

import jax
import jax.numpy as jnp
from jax import lax
from jax.experimental import pallas as pl
from jax.experimental.pallas import tpu as pltpu
from jax.sharding import PartitionSpec as P

HD = 64
WIDE = 256
EPS = 1e-05
LOG2E = math.log2(math.e)
SCALE = 1.0 / math.sqrt(HD)
F32 = jnp.float32
BF = jnp.bfloat16
NT = (((1,), (1,)), ((), ()))
NN = (((1,), (0,)), ((), ()))
TN = (((0,), (0,)), ((), ()))
MESH = pl.DeviceIdType.MESH


def dot(a, b, dims=NN):
    return lax.dot_general(a, b, dims, preferred_element_type=F32)


def lanes(shape):
    return lax.broadcasted_iota(jnp.int32, shape, 1)


def split3(x):
    hi = x.astype(BF).astype(F32)
    mid = (x - hi).astype(BF).astype(F32)
    return hi, mid, x - hi - mid


def partner(x):
    width = x.shape[1]
    first = lanes(x.shape) % HD < HD // 2
    return jnp.where(first, pltpu.roll(x, width - HD // 2, 1), pltpu.roll(x, HD // 2, 1))


def angle_tables(length):
    half = HD // 2
    lane = lax.optimization_barrier(lax.iota(jnp.int32, 2 * HD))
    freqs = 10000.0 ** (-((lane % half).astype(F32) * 2.0 / HD))
    angles = lax.iota(F32, length)[:, None] * freqs[None, :]
    sign = jnp.where(lane % HD < half, -1.0, 1.0)
    return jnp.cos(angles), jnp.sin(angles) * sign[None, :]


def project_kernel(width, x_ref, wq_ref, wk_ref, wv_ref, cos_ref, sin_ref, q_ref, k_ref, v_ref):
    x = x_ref[...]
    cosine = jnp.tile(cos_ref[...], (1, width // (2 * HD)))
    sine = jnp.tile(sin_ref[...], (1, width // (2 * HD)))
    for w_ref, out_ref in ((wq_ref, q_ref), (wk_ref, k_ref)):
        raw = dot(x, w_ref[...])
        out_ref[...] = (raw * cosine + partner(raw) * sine).astype(BF)
    v_ref[...] = dot(x, wv_ref[...]).astype(BF)


def project(rows, w_query, w_key, w_value, cosine, sine, block=512):
    n, depth = rows.shape
    width = w_query.shape[1]
    whole = pl.BlockSpec((depth, width), lambda i: (0, 0))
    table = pl.BlockSpec((block, 2 * HD), lambda i: (i, 0))
    out = pl.BlockSpec((block, width), lambda i: (i, 0))
    return pl.pallas_call(
        functools.partial(project_kernel, width),
        out_shape=(jax.ShapeDtypeStruct((n, width), BF),) * 3,
        grid=(n // block,),
        in_specs=[pl.BlockSpec((block, depth), lambda i: (i, 0)), whole, whole, whole, table, table],
        out_specs=(out, out, out),
        compiler_params=pltpu.CompilerParams(vmem_limit_bytes=40 << 20),
        cost_estimate=pl.CostEstimate(
            flops=2 * n * depth * 3 * width, bytes_accessed=2 * (n * depth + 3 * n * width), transcendentals=0
        ),
        name="project",
    )(rows, w_query, w_key, w_value, cosine, sine)


def own_lanes(h, shape):
    lane = lanes(shape)
    off = lax.rem(lane - h * HD + shape[1], shape[1])
    return off < HD, off


def attend(q, k, v):
    scores = dot(q, k, NT)
    peak = jnp.max(scores, axis=1, keepdims=True)
    return dot(jnp.exp2(scores - peak).astype(BF), v), peak


def query_operand(h, q):
    own, off = own_lanes(h, q.shape)
    q = jnp.where(own, q.astype(F32), 0.0) * (LOG2E * SCALE)
    high = q.astype(BF).astype(F32)
    return high + pltpu.roll(q - high, HD, 1), own, off - 2 * HD


def differ(a, b, bits):
    return sum(lax.rem(a // (1 << k) + b // (1 << k), 2) * (1 << k) for k in range(bits))


def remote(src, dst, send, recv, **to):
    return pltpu.make_async_remote_copy(
        src_ref=src, dst_ref=dst, send_sem=send, recv_sem=recv, device_id=to, device_id_type=MESH
    )


def ring(n, step):
    return lax.rem(lax.axis_index("tensor") + step, n)


def same_core(s, chips):
    me = lax.axis_index("dp")
    return differ(me // 2, s, chips.bit_length() - 1) * 2 + lax.rem(me, 2)


def sibling():
    me = lax.axis_index("dp")
    return me + 1 - 2 * lax.rem(me, 2)


def greet(n, chips, both_cores=False):
    barrier = pltpu.get_barrier_semaphore()
    if both_cores:
        pl.semaphore_signal(barrier, inc=1, device_id={"dp": sibling()}, device_id_type=MESH)
    for step in range(1, n):
        pl.semaphore_signal(barrier, inc=1, device_id={"tensor": ring(n, step)}, device_id_type=MESH)
    for s in range(1, chips):
        pl.semaphore_signal(
            barrier, inc=1, device_id={"dp": same_core(s, chips)}, device_id_type=MESH
        )
    pl.semaphore_wait(barrier, n + chips - 2 + both_cores)


def att_fwd_kernel(
    n, chips, limit_ref, q_ref, k_ref, v_ref, gb_ref, wo_ref,
    ctx_ref, lse_ref, out_ref, gb_all, wo_z, wo_all, ka, va, send_sem, recv_sem, own_sem,
    gs_send, gs_recv, gr_send, gr_recv, wz_send, wz_recv, ws_send, ws_recv, wr_send, wr_recv, keep_sem,
):
    s = pl.program_id(0)
    h = pl.program_id(1)
    heads = pl.num_programs(1)
    rows = q_ref.shape[0] // n
    me = lax.axis_index("tensor")
    place = lax.axis_index("dp")
    core = lax.rem(place, 2)
    bits = chips.bit_length() - 1
    limit = limit_ref[0]

    def spread_gb(c):
        return remote(
            gb_ref, gb_all.at[place // 2, core], gs_send.at[c], gs_recv.at[c], dp=same_core(c, chips)
        )

    def relay_gb(c):
        there = gb_all.at[differ(place // 2, c, bits), core]
        return remote(
            there if c else gb_ref, there, gr_send.at[c], gr_recv.at[c], dp=sibling()
        )

    def wo_over(step):
        return remote(
            wo_ref, wo_z.at[me], wz_send.at[step], wz_recv.at[step], tensor=ring(n, step + 1)
        )

    def spread_wo(c):
        return remote(
            wo_z, wo_all.at[:, place], ws_send.at[c], ws_recv.at[c], dp=same_core(c, chips)
        )

    def relay_wo(c):
        there = wo_all.at[:, differ(place // 2, c, bits) * 2 + core]
        return remote(there if c else wo_z, there, wr_send.at[c], wr_recv.at[c], dp=sibling())

    keeps = [
        pltpu.make_async_copy(gb_ref, gb_all.at[place // 2, core], keep_sem.at[0]),
        pltpu.make_async_copy(wo_ref, wo_z.at[me], keep_sem.at[1]),
        pltpu.make_async_copy(wo_z, wo_all.at[:, place], keep_sem.at[2]),
    ]

    @pl.when((s == 0) & (h == 0))
    def _():
        greet(n, chips, True)
        for step in range(n - 1):
            wo_over(step).start()
        keeps[0].start()
        keeps[1].start()
        for c in range(1, chips):
            spread_gb(c).start()
        relay_gb(0).start()

    @pl.when((s == 1) & (h == 0))
    def _():
        for step in range(n - 1):
            wo_over(step).wait()
        keeps[1].wait()
        for c in range(1, chips):
            spread_wo(c).start()
        relay_wo(0).start()
        keeps[2].start()

    @pl.when((s == n - 2) & (h == 0))
    def _():
        for c in range(1, chips // 2 + 1):
            spread_gb(c).wait_recv()
            relay_gb(c).start()

    @pl.when((s == n - 1) & (h == 0))
    def _():
        for c in range(1, chips):
            spread_wo(c).wait_recv()
            relay_wo(c).start()
        for c in range(chips // 2 + 1, chips):
            spread_gb(c).wait_recv()
            relay_gb(c).start()

    @pl.when(s == 0)
    def _():
        own, off = own_lanes(h, k_ref.shape)
        k = jnp.where(own, k_ref[...].astype(F32), 0.0)
        row = lax.broadcasted_iota(jnp.int32, k.shape, 0)
        bias = jnp.where(row < limit, 0.0, -1e30)
        ka[h] = jnp.where(off == 2 * HD, bias, k + pltpu.roll(k, HD, 1)).astype(BF)
        v = jnp.where(own, v_ref[...].astype(F32), 0.0)
        va[h] = jnp.where(off == HD, 1.0, v).astype(BF)

    owner = ring(n, s + 1)
    block = pl.ds(pl.multiple_of(owner * rows, rows), rows)
    q, own, off = query_operand(h, q_ref[block, :])
    acc, peak = attend(jnp.where(off == 0, 1.0, q).astype(BF), ka[h], va[h])
    total = jnp.sum(jnp.where(off == -HD, acc, 0.0), axis=1, keepdims=True)
    out = (acc * (1.0 / total)).astype(BF)
    ctx_ref[block, :] = jnp.where(own, out, ctx_ref[block, :])
    lse_ref[block, :] = jnp.where(
        lanes((rows, 128)) == h, peak + jnp.log2(total), lse_ref[block, :]
    )

    def push(step):
        return pltpu.make_async_remote_copy(
            src_ref=ctx_ref.at[block],
            dst_ref=out_ref.at[me],
            send_sem=send_sem.at[step],
            recv_sem=recv_sem.at[step],
            device_id={"tensor": owner},
            device_id_type=MESH,
        )

    @pl.when((h == heads - 1) & (s < n - 1))
    def _():
        push(s).start()

    @pl.when((h == heads - 1) & (s == n - 1))
    def _():
        keep = pltpu.make_async_copy(ctx_ref.at[block], out_ref.at[me], own_sem)
        keep.start()
        for step in range(n - 1):
            push(step).wait()
        keep.wait()
        keeps[0].wait()
        keeps[2].wait()
        for c in range(chips):
            relay_gb(c).wait()
            relay_wo(c).wait()
            if c:
                spread_gb(c).wait_send()
                spread_wo(c).wait_send()


def att_fwd(q, k, v, grad_rows, w_out_piece, limit, heads, n, devices):
    total, width = q.shape
    rows = total // n
    depth = grad_rows.shape[1]
    share = w_out_piece.shape[0]
    chips = devices // 2
    hbm = pl.BlockSpec(memory_space=pl.ANY)

    def whole(d):
        return pl.BlockSpec((total, d), lambda *_: (0, 0), pipeline_mode=pl.Buffered(1))

    return pl.pallas_call(
        functools.partial(att_fwd_kernel, n, chips),
        out_shape=(
            jax.ShapeDtypeStruct((total, width), BF),
            jax.ShapeDtypeStruct((total, 128), F32),
            jax.ShapeDtypeStruct((n, rows, width), BF),
            jax.ShapeDtypeStruct((chips, 2, rows, depth), BF),
            jax.ShapeDtypeStruct((n, share, depth), BF),
            jax.ShapeDtypeStruct((n, devices, share, depth), BF),
        ),
        grid_spec=pltpu.PrefetchScalarGridSpec(
            num_scalar_prefetch=1,
            grid=(n, heads),
            in_specs=[whole(width)] * 3 + [hbm] * 2,
            out_specs=[whole(width), whole(128)] + [hbm] * 4,
            scratch_shapes=[pltpu.VMEM((heads, total, width), BF)] * 2
            + [pltpu.SemaphoreType.DMA((n - 1,))] * 2
            + [pltpu.SemaphoreType.DMA]
            + [pltpu.SemaphoreType.DMA((chips,))] * 4
            + [pltpu.SemaphoreType.DMA((n - 1,))] * 2
            + [pltpu.SemaphoreType.DMA((chips,))] * 4
            + [pltpu.SemaphoreType.DMA((3,))],
        ),
        compiler_params=pltpu.CompilerParams(
            vmem_limit_bytes=56 << 20, collective_id=1, has_side_effects=True
        ),
        cost_estimate=pl.CostEstimate(
            flops=4 * total * total * 256 * heads,
            bytes_accessed=10 * total * width,
            transcendentals=total * total * heads,
        ),
        name="att_fwd",
    )(limit, q, k, v, grad_rows, w_out_piece)


def att_bwd_kernel(
    n, bk, chips, heads, limit_ref, ga_ref, wo_ref, parts_ref, q_ref, k_ref, v_ref, ctx_ref, lse_ref,
    cos_ref, sin_ref, pk_ref, own_ref, sums_ref, do, gc, ka, va, dka, dva, dqs, dvs,
    send_sem, recv_sem, out_send, out_recv, pk_send, pk_recv, keep_sem,
):
    h = pl.program_id(0)
    t = pl.program_id(1)
    total, width = k_ref.shape
    rows = total // n
    me = lax.axis_index("tensor")
    limit = limit_ref[0]
    mine = pl.ds(pl.multiple_of(me * rows, rows), rows)
    to_first = lax.rem(width - h * HD, width)

    def push(step):
        return remote(
            gc.at[step], do.at[mine], send_sem.at[step], recv_sem.at[step], tensor=ring(n, step + 1)
        )

    def push_out(s):
        return remote(
            parts_ref.at[s], sums_ref.at[s - 1], out_send.at[s - 1], out_recv.at[s - 1],
            dp=same_core(s, chips),
        )

    def columns(slot):
        return pl.ds(pl.multiple_of(slot * 128, 128), 128)

    def push_pack(slot, step):
        owner = ring(n, step + 1)
        return remote(
            pk_ref.at[pl.ds(pl.multiple_of(owner * rows, rows), rows), columns(slot)],
            own_ref.at[me, :, columns(slot)],
            pk_send.at[slot, step], pk_recv.at[slot, step], tensor=owner,
        )

    def keep(slot):
        return pltpu.make_async_copy(
            pk_ref.at[mine, columns(slot)], own_ref.at[me, :, columns(slot)], keep_sem.at[slot]
        )

    def send_pack(slot):
        for step in range(n - 1):
            push_pack(slot, step).start()
        keep(slot).start()

    @pl.when((h == 0) & (t == 0))
    def _():
        greet(n, chips)
        for s in range(1, chips):
            push_out(s).start()

        def send(step, carry):
            gc[step] = dot(ga_ref[...], wo_ref[ring(n, step + 1)], NT).astype(BF)
            push(step).start()
            return carry

        lax.fori_loop(0, n - 1, send, 0)
        do[mine, :] = dot(ga_ref[...], wo_ref[me], NT).astype(BF)

    @pl.when((h == 0) & (t > 0))
    def _():
        push(t - 1).wait_recv()

    @pl.when(t == 0)
    def _():
        lane = lanes((total, width))
        row = lax.broadcasted_iota(jnp.int32, (total, width), 0)
        k = jnp.where(lane < HD, pltpu.roll(k_ref[...].astype(F32), to_first, 1), 0.0)
        k = jnp.where(
            lane == 2 * HD + 3, jnp.where(row < limit, 0.0, -1e30), k + pltpu.roll(k, HD, 1)
        )
        ones = (lane >= 2 * HD) & (lane < 2 * HD + 3)
        ka[...] = jnp.where(ones, 1.0, k).astype(BF)
        v = jnp.where(lane < HD, pltpu.roll(v_ref[...].astype(F32), to_first, 1), 0.0)
        va[...] = jnp.where(ones, 1.0, v).astype(BF)
        dka[...] = jnp.zeros_like(dka)
        dva[...] = jnp.zeros_like(dva)

    source = ring(n, n - t)
    block = pl.ds(pl.multiple_of(source * rows, rows), rows)
    off = lanes((rows, width)) - 2 * HD
    q = pltpu.roll(q_ref[block, :].astype(F32), to_first, 1) * (LOG2E * SCALE)
    q = jnp.where(off < -HD, q, 0.0)
    high = q.astype(BF).astype(F32)
    q = high + pltpu.roll(q - high, HD, 1)
    logsum = jnp.sum(
        jnp.where(lanes((rows, 128)) == h, lse_ref[block, :], 0.0), axis=1, keepdims=True
    )
    a, b, c = split3(-logsum)
    q = jnp.where(off == 0, a, jnp.where(off == 1, b, jnp.where(off == 2, c, q)))
    q = jnp.where(off == 3, 1.0, q).astype(BF)
    g = jnp.where(off < -HD, pltpu.roll(do[block, :].astype(F32), to_first, 1), 0.0)
    delta = jnp.sum(
        g * pltpu.roll(ctx_ref[block, :].astype(F32), to_first, 1), axis=1, keepdims=True
    )
    a, b, c = split3(-delta)
    g = jnp.where(off == 0, a, jnp.where(off == 1, b, jnp.where(off == 2, c, g))).astype(BF)
    acc = jnp.zeros((rows, width), F32)
    for j in range(total // bk):
        rk = pl.ds(j * bk, bk)
        kt = ka[rk, :]
        probs = jnp.exp2(dot(kt, q, NT))
        grad = (probs * dot(va[rk, :], g, NT)).astype(BF)
        dva[rk, :] += dot(probs.astype(BF), g)
        dka[rk, :] += dot(grad, q)
        acc = acc + dot(grad, kt, TN)
    dqs[block, :] = acc[:, :128] * SCALE

    @pl.when(t == n - 1)
    def _():
        first = lanes((total, 128)) < HD
        dk = dka[:, :128]
        grad = jnp.where(first, dqs[...], (dk + pltpu.roll(dk, HD, 1)) * (1.0 / LOG2E))
        grad = grad * cos_ref[...] - partner(grad) * sin_ref[...]
        pk_ref[:, columns(h)] = grad.astype(BF)
        send_pack(h)

        @pl.when(lax.rem(h, 2) == 0)
        def _():
            dvs[...] = dva[:, :128]

        @pl.when(lax.rem(h, 2) == 1)
        def _():
            both = jnp.where(first, dvs[...], pltpu.roll(dva[:, :128], HD, 1))
            pk_ref[:, columns(heads + h // 2)] = both.astype(BF)
            send_pack(heads + h // 2)

    @pl.when((t == n - 1) & (h == heads - 1))
    def _():
        for step in range(n - 1):
            push(step).wait_send()
        for s in range(1, chips):
            push_out(s).wait()
        for slot in range(heads + heads // 2):
            keep(slot).wait()
            for step in range(n - 1):
                push_pack(slot, step).wait()


def att_bwd(grad_attn, w_out, parts, q, k, v, ctx, lse, limit, cosine, sine, heads, n, bk=512):
    total, width = q.shape
    rows, depth = grad_attn.shape
    chips = parts.shape[0]
    slots = heads + heads // 2
    hbm = pl.BlockSpec(memory_space=pl.ANY)

    def whole(*shape):
        return pl.BlockSpec(shape, lambda *_: (0,) * len(shape), pipeline_mode=pl.Buffered(1))

    return pl.pallas_call(
        functools.partial(att_bwd_kernel, n, bk, chips, heads),
        out_shape=(
            jax.ShapeDtypeStruct((total, slots * 128), BF),
            jax.ShapeDtypeStruct((n, rows, slots * 128), BF),
            jax.ShapeDtypeStruct((chips - 1, rows, depth), BF),
        ),
        grid_spec=pltpu.PrefetchScalarGridSpec(
            num_scalar_prefetch=1,
            grid=(heads, n),
            in_specs=[whole(rows, depth), whole(n, width, depth), hbm]
            + [whole(total, width)] * 4
            + [whole(total, 128)] * 3,
            out_specs=[whole(total, slots * 128), hbm, hbm],
            scratch_shapes=[
                pltpu.VMEM((total, width), BF),
                pltpu.VMEM((n - 1, rows, width), BF),
                pltpu.VMEM((total, width), BF),
                pltpu.VMEM((total, width), BF),
                pltpu.VMEM((total, width), F32),
                pltpu.VMEM((total, width), F32),
                pltpu.VMEM((total, 128), F32),
                pltpu.VMEM((total, 128), F32),
            ]
            + [pltpu.SemaphoreType.DMA((n - 1,))] * 2
            + [pltpu.SemaphoreType.DMA((chips - 1,))] * 2
            + [pltpu.SemaphoreType.DMA((slots, n - 1))] * 2
            + [pltpu.SemaphoreType.DMA((slots,))],
        ),
        compiler_params=pltpu.CompilerParams(
            vmem_limit_bytes=56 << 20, collective_id=2, has_side_effects=True
        ),
        cost_estimate=pl.CostEstimate(
            flops=10 * total * total * 256 * heads,
            bytes_accessed=20 * total * width,
            transcendentals=total * total * heads,
        ),
        name="att_bwd",
    )(limit, grad_attn, w_out, parts, q, k, v, ctx, lse, cosine, sine)


def finish_kernel(
    chips, n, width, x_ref, pk_ref, own_ref, w_ref, tokens_ref, middle_ref, gain_ref, vec_ref,
    input_ref, q_ref, k_ref, v_ref, sums_ref,
    full, mate, sib, land, fin, every, vec_z, vec_dp, vec_me,
    sx_send, sx_recv, rs_send, rs_recv, ag_send, ag_recv, rl_send, rl_recv,
    vz_send, vz_recv, vd_send, vd_recv, own_sem,
):
    bits = chips.bit_length() - 1
    me = lax.axis_index("dp")
    place = lax.axis_index("tensor")
    core = lax.rem(me, 2)
    chip = me // 2
    other = 1 - core
    heads = width // HD
    piece = fin.shape[0]

    def swap(s):
        return remote(mate.at[s], sib.at[s], sx_send.at[s], sx_recv.at[s], dp=chip * 2 + other)

    def push(s):
        return remote(sib.at[s], land.at[s], rs_send.at[s], rs_recv.at[s], dp=same_core(s, chips))

    def spread(s):
        return remote(
            fin, every.at[chip, core], ag_send.at[s], ag_recv.at[s], dp=same_core(s, chips)
        )

    def relay(s):
        src = every.at[differ(chip, s, bits), core]
        return remote(src, src, rl_send.at[s], rl_recv.at[s], dp=chip * 2 + other)

    def vec_over(step):
        return remote(
            vec_me.at[0], vec_z.at[place], vz_send.at[step], vz_recv.at[step], tensor=ring(n, step + 1)
        )

    def vec_across(step):
        return remote(
            vec_me.at[1], vec_dp.at[me], vd_send.at[step], vd_recv.at[step],
            dp=lax.rem(me + step + 1, 2 * chips),
        )

    barrier = pltpu.get_barrier_semaphore()
    for step in range(n - 1):
        pl.semaphore_signal(barrier, inc=1, device_id={"tensor": ring(n, step + 1)}, device_id_type=MESH)
    for step in range(2 * chips - 1):
        to = lax.rem(me + step + 1, 2 * chips)
        pl.semaphore_signal(barrier, inc=1, device_id={"dp": to}, device_id_type=MESH)

    full[...] = dot(x_ref[...], pk_ref[...], TN)
    pl.semaphore_wait(barrier, n + 2 * chips - 2)

    def part(s, which):
        start = (differ(chip, s, bits) * 2 + which) * piece
        return full[pl.ds(pl.multiple_of(start, piece), piece), :]

    for s in range(chips):
        mate[s] = part(s, other).astype(BF)
        swap(s).start()

    grad = jnp.zeros(input_ref.shape, F32)
    for t in range(n):
        grad = grad + dot(own_ref[t], w_ref[t]).astype(BF).astype(F32)

    for s in range(1, chips):
        swap(s).wait_recv()
        sib[s] = (sib[s].astype(F32) + part(s, core)).astype(BF)
        push(s).start()
    swap(0).wait_recv()
    total = sib[0].astype(F32) + part(0, core)

    values = tokens_ref[...].astype(F32)
    values = values - jnp.mean(values, axis=1, keepdims=True)
    inverse = lax.rsqrt(jnp.mean(values * values, axis=1, keepdims=True) + EPS)
    scaled = values * inverse
    through = grad * gain_ref[...]
    inner = through - jnp.mean(through, axis=1, keepdims=True)
    inner = inner - scaled * jnp.mean(through * scaled, axis=1, keepdims=True)
    input_ref[...] = middle_ref[...] + inverse * inner
    vec_me[0, 0:1] = jnp.sum(grad * scaled, axis=0, keepdims=True)
    vec_me[0, 1:2] = jnp.sum(grad, axis=0, keepdims=True)
    vec_me[0, 2:4] = vec_ref[...]
    vec_me[0, 4:8] = jnp.zeros((4, vec_ref.shape[1]), F32)
    vec_z[place] = vec_me[0]
    for step in range(n - 1):
        vec_over(step).start()

    for s in range(1, chips):
        push(s).wait_recv()
        total = total + land[s].astype(F32)
    fin[...] = total.astype(BF)
    for s in range(1, chips):
        spread(s).start()
    mine = pltpu.make_async_copy(fin, every.at[chip, core], own_sem)
    mine.start()
    mine.wait()
    relay(0).start()

    for step in range(n - 1):
        vec_over(step).wait()
    vec = vec_z[0]
    for t in range(1, n):
        vec = vec + vec_z[t]
    vec_me[1] = vec
    vec_dp[me] = vec
    for step in range(2 * chips - 1):
        vec_across(step).start()
    for s in range(1, chips):
        spread(s).wait_recv()
        relay(s).start()
    for step in range(2 * chips - 1):
        vec_across(step).wait()
    vec = vec_dp[0]
    for t in range(1, 2 * chips):
        vec = vec + vec_dp[t]
    sums_ref[...] = vec
    for s in range(chips):
        relay(s).wait()
        swap(s).wait_send()
        if s > 0:
            spread(s).wait_send()
            push(s).wait_send()
    first = lanes((piece, 128)) < HD
    for d in range(2 * chips):
        rows = slice(d * piece, (d + 1) * piece)
        g = every[d // 2, d % 2].astype(F32)
        for pair in range(heads // 2):
            a = g[:, pair * 256 : pair * 256 + 128]
            b = g[:, pair * 256 + 128 : pair * 256 + 256]
            out = slice(pair * 128, pair * 128 + 128)
            q_ref[rows, out] = jnp.where(first, a, pltpu.roll(b, HD, 1))
            k_ref[rows, out] = jnp.where(first, pltpu.roll(a, HD, 1), b)
            v_ref[rows, out] = g[:, (heads + pair) * 128 : (heads + pair + 1) * 128]


def finish(rows_all, packed, own, w_all, tokens, middle, gain, vec, width, devices):
    n, rows, packs = own.shape
    depth = tokens.shape[1]
    chips = devices // 2
    piece = depth // devices
    vmem = pl.BlockSpec(memory_space=pltpu.VMEM)
    out = jax.ShapeDtypeStruct((depth, width), F32)
    return pl.pallas_call(
        functools.partial(finish_kernel, chips, n, width),
        out_shape=(
            jax.ShapeDtypeStruct((rows, depth), F32), out, out, out,
            jax.ShapeDtypeStruct((8, depth), F32),
        ),
        in_specs=[vmem] * 8,
        out_specs=[vmem] * 5,
        scratch_shapes=[
            pltpu.VMEM((depth, packs), F32),
            pltpu.VMEM((chips, piece, packs), BF),
            pltpu.VMEM((chips, piece, packs), BF),
            pltpu.VMEM((chips, piece, packs), BF),
            pltpu.VMEM((piece, packs), BF),
            pltpu.VMEM((chips, 2, piece, packs), BF),
            pltpu.VMEM((n, 8, depth), F32),
            pltpu.VMEM((devices, 8, depth), F32),
            pltpu.VMEM((2, 8, depth), F32),
        ]
        + [pltpu.SemaphoreType.DMA((chips,))] * 8
        + [pltpu.SemaphoreType.DMA((n - 1,))] * 2
        + [pltpu.SemaphoreType.DMA((devices - 1,))] * 2
        + [pltpu.SemaphoreType.DMA],
        compiler_params=pltpu.CompilerParams(
            vmem_limit_bytes=56 << 20, collective_id=4, has_side_effects=True
        ),
        cost_estimate=pl.CostEstimate(
            flops=4 * n * rows * depth * packs, bytes_accessed=20 << 20, transcendentals=0
        ),
        name="finish",
    )(rows_all, packed, own, w_all, tokens, middle, gain.reshape(1, depth), vec)


def ffn_kernel(
    chips, x_ref, gb_ref, w_ref, dx_ref, out_ref, dw_ref,
    rows_all, gb, hid, gate_g, up_g, own, sib, mate, acc,
    ag_send, ag_recv, rl_send, rl_recv, sx_send, sx_recv, rs_send, rs_recv, gb_sem, out_sem, dx_sem,
):
    bits = chips.bit_length() - 1
    me = lax.axis_index("dp")
    core = lax.rem(me, 2)
    chip = me // 2
    other = 1 - core
    rows, depth = x_ref.shape
    n = dw_ref.shape[0]
    share = dw_ref.shape[2]

    def spread(s):
        to = differ(chip, s, bits) * 2 + core
        return remote(x_ref, rows_all.at[chip, core], ag_send.at[s], ag_recv.at[s], dp=to)

    def relay(s):
        src = differ(chip, s, bits)
        return remote(
            rows_all.at[src, core], rows_all.at[src, core], rl_send.at[s], rl_recv.at[s],
            dp=chip * 2 + other,
        )

    def swap(s):
        return remote(
            mate.at[lax.rem(s, 2)], sib.at[s], sx_send.at[s], sx_recv.at[s], dp=chip * 2 + other
        )

    def push(s):
        to = differ(chip, s, bits) * 2 + core
        return remote(sib.at[s, 0], dx_ref.at[s], rs_send.at[s], rs_recv.at[s], dp=to)

    def fetch(s):
        slot = lax.rem(s, 2)
        return pltpu.make_async_copy(
            gb_ref.at[differ(chip, s, bits)], gb.at[slot], gb_sem.at[slot]
        )

    def keep(s):
        return pltpu.make_async_copy(sib.at[s, 1], out_ref.at[s], out_sem.at[s])

    fetch(0).start()
    barrier = pltpu.get_barrier_semaphore()
    pl.semaphore_signal(barrier, inc=1, device_id={"dp": chip * 2 + other}, device_id_type=MESH)
    for s in range(1, chips):
        to = differ(chip, s, bits) * 2 + core
        pl.semaphore_signal(barrier, inc=1, device_id={"dp": to}, device_id_type=MESH)
    pl.semaphore_wait(barrier, chips)
    for s in range(1, chips):
        spread(s).start()
    mine = pltpu.make_async_copy(x_ref, rows_all.at[chip, core], ag_send.at[0])
    mine.start()
    mine.wait()
    relay(0).start()
    acc[...] = jnp.zeros_like(acc)

    def shard(src, slot, which, put):
        x = rows_all[src, which]
        grad = gb[slot, which]
        gate = dot(x, w_ref[0], NT)
        upper = dot(x, w_ref[1], NT)
        grad_hidden = dot(grad, w_ref[2], NT)
        sigma = jax.nn.sigmoid(gate)
        act = gate * sigma
        part = pl.ds(pl.multiple_of(which * rows, rows), rows)
        hidden = (act * upper).astype(BF)
        grad_gate = (grad_hidden * upper * sigma * (1.0 + gate * (1.0 - sigma))).astype(BF)
        grad_upper = (grad_hidden * act).astype(BF)
        hid[part, :] = hidden
        gate_g[part, :] = grad_gate
        up_g[part, :] = grad_upper
        put[0] = (dot(grad_gate, w_ref[0]) + dot(grad_upper, w_ref[1])).astype(BF)
        put[1] = dot(hidden, w_ref[2]).astype(BF)

    def step(s, carry):
        src = differ(chip, s, bits)
        slot = lax.rem(s, 2)
        relay(s).wait_recv()
        fetch(s).wait()

        @pl.when(s < chips - 1)
        def _():
            fetch(s + 1).start()

        @pl.when(s >= 2)
        def _():
            swap(s - 2).wait_send()

        shard(src, slot, other, mate.at[slot])
        swap(s).start()
        shard(src, slot, core, own)
        swap(s).wait_recv()
        for k in range(2):
            sib[s, k] = (sib[s, k].astype(F32) + own[k].astype(F32)).astype(BF)

        @pl.when(s > 0)
        def _():
            push(s).start()

        keep(s).start()

        @pl.when(s < chips - 1)
        def _():
            spread(s + 1).wait_recv()
            relay(s + 1).start()

        x = rows_all[src].reshape(2 * rows, depth)
        acc[0] += dot(gate_g[...], x, TN)
        acc[1] += dot(up_g[...], x, TN)
        acc[2] += dot(hid[...], gb[slot].reshape(2 * rows, depth), TN)
        return carry

    lax.fori_loop(0, chips, step, 0)
    first = pltpu.make_async_copy(sib.at[0, 0], dx_ref.at[0], dx_sem)
    first.start()
    for t in range(n):
        for k in range(3):
            dw_ref[t, k] = acc[k, t * share : (t + 1) * share, :].astype(BF)
    first.wait()
    for s in range(chips):
        keep(s).wait()
        relay(s).wait_send()
        if s >= chips - 2:
            swap(s).wait_send()
        if s > 0:
            spread(s).wait_send()
            push(s).wait()


def ffn(x, grad_branch, weights, n, devices):
    rows, depth = x.shape
    chips = devices // 2
    hidden = weights.shape[1]
    share = hidden // n
    vmem = pl.BlockSpec(memory_space=pltpu.VMEM)
    hbm = pl.BlockSpec(memory_space=pl.ANY)
    return pl.pallas_call(
        functools.partial(ffn_kernel, chips),
        out_shape=(
            jax.ShapeDtypeStruct((chips, rows, depth), BF),
            jax.ShapeDtypeStruct((chips, rows, depth), BF),
            jax.ShapeDtypeStruct((n, 3, share, depth), BF),
        ),
        in_specs=[vmem, hbm, vmem],
        out_specs=[hbm, hbm, vmem],
        scratch_shapes=[
            pltpu.VMEM((chips, 2, rows, depth), BF),
            pltpu.VMEM((2, 2, rows, depth), BF),
        ]
        + [pltpu.VMEM((2 * rows, hidden), BF)] * 3
        + [
            pltpu.VMEM((2, rows, depth), BF),
            pltpu.VMEM((chips, 2, rows, depth), BF),
            pltpu.VMEM((2, 2, rows, depth), BF),
            pltpu.VMEM((3, hidden, depth), F32),
        ]
        + [pltpu.SemaphoreType.DMA((chips,))] * 8
        + [pltpu.SemaphoreType.DMA((2,)), pltpu.SemaphoreType.DMA((chips,)), pltpu.SemaphoreType.DMA],
        compiler_params=pltpu.CompilerParams(
            vmem_limit_bytes=60 << 20, collective_id=3, has_side_effects=True
        ),
        cost_estimate=pl.CostEstimate(
            flops=2 * 9 * devices * rows * depth * hidden, bytes_accessed=30 << 20, transcendentals=0
        ),
        name="ffn",
    )(x, grad_branch, weights)


def norm_parts(values):
    centre = jnp.mean(values, axis=-1, keepdims=True)
    centred = values - centre
    inverse = lax.rsqrt(jnp.mean(centred * centred, axis=-1, keepdims=True) + EPS)
    return centred * inverse, inverse


def norm_back(upstream, scaled, inverse, gain):
    through = upstream * gain
    inner = (
        through
        - jnp.mean(through, axis=-1, keepdims=True)
        - scaled * jnp.mean(through * scaled, axis=-1, keepdims=True)
    )
    return inverse * inner, jnp.sum(upstream * scaled, axis=0), jnp.sum(upstream, axis=0)


def pack_weights(w_query, w_key, w_value):
    depth, width = w_query.shape
    query, key = (w.T.reshape(width // HD, 1, HD, depth) for w in (w_query, w_key))
    both = jnp.concatenate([query, key], axis=1).reshape(2 * width, depth)
    return jnp.concatenate([both, w_value.T], axis=0)


def on_device(
    tokens, lengths, ln1_gain, ln1_bias, w_query, w_key, w_value, w_out,
    ln2_gain, ln2_bias, w_gate, w_up, down_weight, cotangent,
):
    n = lax.axis_size("tensor")
    local_rows, depth = tokens.shape
    length = local_rows * n
    width = w_query.shape[1]
    heads = width // HD
    row_ids = lax.axis_index("tensor") * local_rows + lax.iota(jnp.int32, local_rows)
    valid = (row_ids < lengths[0])[:, None]

    def gather(x):
        return lax.all_gather(x, "tensor", axis=0, tiled=True)

    def padded(x):
        return x if width >= WIDE else jnp.pad(x, ((0, 0), (0, WIDE - width)))

    inputs = tokens.astype(F32)
    scaled1, _ = norm_parts(inputs)
    attn_rows = gather((scaled1 * ln1_gain + ln1_bias).astype(BF))
    cosine, sine = angle_tables(length)
    grad_out = jnp.where(valid, cotangent.astype(F32), 0.0)
    devices = lax.axis_size("dp")
    place = lax.axis_index("dp")
    share = w_gate.shape[1] // devices

    def piece(x, axis):
        return lax.dynamic_slice_in_dim(x, place * share, share, axis)

    weights = jnp.stack([piece(w_gate, 1).T, piece(w_up, 1).T, piece(down_weight, 0)])
    weights = lax.all_gather(weights, "tensor", axis=1, tiled=True)
    q, k, v = project(attn_rows, w_query, w_key, w_value, cosine, sine)
    q, k, v = padded(q), padded(k), padded(v)
    context, logsum, context_own, grad_branch, _, w_out_all = att_fwd(
        q, k, v, grad_out.astype(BF),
        lax.dynamic_slice_in_dim(w_out, place * (width // devices), width // devices, 0),
        lengths, heads, n, devices,
    )
    w_out_all = w_out_all.reshape(n, width, depth)
    if width < WIDE:
        w_out_all = jnp.pad(w_out_all, ((0, 0), (0, WIDE - width), (0, 0)))
    attn_out = sum(dot(context_own[t], w_out_all[t]).astype(BF).astype(F32) for t in range(n))
    middle = inputs + attn_out
    scaled2, inverse2 = norm_parts(middle)
    ffn_in = (scaled2 * ln2_gain + ln2_bias).astype(BF)
    w_packed, ffn_in = lax.optimization_barrier(
        (pack_weights(w_query, w_key, w_value), ffn_in)
    )
    w_packed = lax.all_gather(w_packed, "tensor", axis=0)
    grad_parts, out_parts, ffn_grads = ffn(ffn_in, grad_branch, weights, n, devices)
    grad_ffn_in = sum(grad_parts[p].astype(F32) for p in range(devices // 2))
    grad_norm2, gain2_grad, shift2_grad = norm_back(
        grad_ffn_in, scaled2, inverse2, ln2_gain
    )
    grad_middle = grad_out + grad_norm2
    grad_attn = grad_middle.astype(BF)
    parts = jnp.stack([dot(context_own[t, :, :width], grad_attn, TN).astype(BF) for t in range(n)])
    parts = parts.reshape(n, devices, width // devices, depth).transpose(1, 0, 2, 3)
    parts = lax.psum_scatter(parts, "dp", scatter_dimension=0, tiled=True)[0]
    grads = jnp.concatenate([ffn_grads.reshape(n, 3 * share, depth), parts], axis=1)
    grads = lax.psum_scatter(grads, "tensor", scatter_dimension=0, tiled=True)[0]
    grads = lax.all_gather(grads, "dp", axis=0)
    gate_grad, up_grad, down_grad = (
        grads[:, k * share : (k + 1) * share].reshape(devices * share, depth).astype(F32)
        for k in range(3)
    )
    gate_grad, up_grad = gate_grad.T, up_grad.T
    out_grad = grads[:, 3 * share :].reshape(width, depth).astype(F32)
    packed, packed_own, out_sums = att_bwd(
        grad_attn, w_out_all, out_parts, q, k, v, context, logsum, lengths, cosine, sine, heads, n
    )
    ffn_out = sum(x.astype(F32) for x in (out_parts[0], *out_sums))
    output = jnp.where(valid, middle + ffn_out, 0.0).astype(BF)
    input_grad, query_grad, key_grad, value_grad, sums = finish(
        attn_rows, packed, packed_own, w_packed, tokens, grad_middle, ln1_gain,
        jnp.stack([gain2_grad, shift2_grad]), width, devices,
    )
    gain1_grad, shift1_grad, gain2_grad, shift2_grad = (sums[i] for i in range(4))
    return (
        output, input_grad, gain1_grad, shift1_grad, query_grad, key_grad, value_grad, out_grad,
        gain2_grad, shift2_grad, gate_grad, up_grad, down_grad,
    )


def solution(mesh):
    rows = P(("dp", "tensor"), None)
    columns = P(None, "tensor")
    parts = P("tensor", None)
    return jax.shard_map(
        on_device,
        mesh=mesh,
        in_specs=(
            rows, P("dp"), P(), P(), columns, columns, columns, parts,
            P(), P(), columns, columns, parts, rows,
        ),
        out_specs=(
            rows, rows, P(), P(), columns, columns, columns, parts,
            P(), P(), columns, columns, parts,
        ),
        check_vma=False,
    )
```

time: 1300 us -> 725 us (0.56)
  waiting for transfers between devices: 667 us -> 174 us
  Pallas kernels: 0 us -> 440 us
  matrix products: 342 us -> 3.97 us
  other arithmetic: 114 us -> 44.2 us
  local copies, waits for them, and re-layouts: 86.3 us -> 40.2 us
  blocking collectives: 39.8 us -> 0 us
  loops' own time: 19 us -> 0 us
    pallas_call x0 -> x5, Pallas kernels: none -> 440 us  [the longest x1 198 us: att_bwd(): pl.pallas_call(functools.partial(att_bwd_kernel, n, bk, chips, heads), ou...]
    dot_general x44 -> x8, matrix products: 342 us -> 3.97 us  [dot(): return lax.dot_general(a, b, dims, preferred_element_type=F32)]
    all_gather x4, waiting for transfers between devices: 266 us -> 68.7 us  [the longest x1 60.4 us: gather(): return lax.all_gather(x, 'tensor', axis=0, tiled=True)]
    reduce_scatter x4 -> x2, waiting for transfers between devices: 280 us -> 104 us  [the longest x1 63.6 us: on_device(): lax.psum_scatter(grads, 'tensor', scatter_dimension=0, tiled=True)[0]]
    psum x1 -> x0, waiting for transfers between devices: 121 us -> none  [on_device(): lax.psum(query_grad.astype(jnp.bfloat16), 'dp').astype(jnp.float32)]
    convert_element_type x15 -> x7, other arithmetic: 68.6 us -> 14.9 us  [the longest x1 3.8 us: on_device(): output = jnp.where(valid, middle + ffn_out, 0.0).astype(BF)]
    dynamic_update_slice x8 -> x0, local copies, waits for them, and re-layouts: 46.4 us -> none  [one_window(): lax.scan(one_step, (zero_rows, zero_rows), jnp.arange(per_window))]
    psum x1 -> x0, blocking collectives: 39.8 us -> none  [on_device(): lax.psum((gain1_grad, shift1_grad, gain2_grad, shift2_grad), ('dp', 'tens...]
  transfers between devices with their start and end apart: 9 -> 6, of which waited for: 9 -> 4; matrix products, arithmetic and copies ran while one was open for 7% -> 4% of each run, Pallas kernels for 0% -> 47%
where the time goes in v1:
time: 725 us; the launch traced here: 717 us
  Pallas kernels  440 us (61%)
  waiting for transfers between devices  174 us (24%)
  other arithmetic  44.2 us (6%)
  local copies, waits for them, and re-layouts  40.2 us (6%)
  between operations  15.6 us (2%)
    pallas_call x1, Pallas kernels, att_bwd(): pl.pallas_call(functools.partial(att_bwd_kernel, n, bk, chips, heads), ou...  198 us
    pallas_call x1, Pallas kernels, ffn(): pl.pallas_call(functools.partial(ffn_kernel, chips), out_shape=(jax.Shape...  100 us
    pallas_call x1, Pallas kernels, att_fwd(): pl.pallas_call(functools.partial(att_fwd_kernel, n, chips), out_shape=(ja...  84 us
    reduce_scatter x1, waiting for transfers between devices, on_device(): lax.psum_scatter(grads, 'tensor', scatter_dimension=0, tiled=True)[0]  63.6 us
    all_gather x1, waiting for transfers between devices, gather(): return lax.all_gather(x, 'tensor', axis=0, tiled=True)  60.4 us
    pallas_call x1, Pallas kernels, finish(): pl.pallas_call(functools.partial(finish_kernel, chips, n, width), out_sha...  51.7 us
    reduce_scatter x1, waiting for transfers between devices, on_device(): parts = lax.psum_scatter(parts, 'dp', scatter_dimension=0, tiled=True)[0]  40.7 us
    unnamed x59, local copies, waits for them, and re-layouts  16.1 us
  transfers between devices with their start and end apart: 6, of which 4 were waited for; matrix products, arithmetic and copies ran while one was open for 4% of the time, Pallas kernels for 47%

profile of v1, /device:TPU:9, one launch (start us, length us, event | category | flops | bytes accessed | tf_op | source)
XLA Modules:
  0.0 717.2 jit_solution(12321598315336396244)
XLA Ops:
  7.3 1.6 convert_reduce_fusion
  8.9 1.6 fusion.2
  10.5 1.4 fusion.5
  12.0 1.1 constant_dynamic-slice_fusion
  13.3 0.9 copy.72
  14.2 2.0 pad_maximum_fusion.3
  16.9 2.0 copy.63
  19.5 1.1 copy.62
  20.6 3.9 sine_multiply_fusion
  24.5 1.6 constant_dynamic-slice_fusion.2.wo_ref
  26.1 2.6 pad_maximum_fusion.1
  28.7 2.5 fusion.9.gb_ref
  31.2 60.4 %all-gather.6.cloned.1.call-done.x_ref = bf16[2048,1024]{1,0:T(8,128)(2,1)} async-done(((bf16[512,1024]{1,0:T(8,128)(2,1)}), bf16[2048,1024]{1,0:T(8,128)(2,1)}) %all-gather.6.cloned.1.call-update) | async-done | bytes 4194320 | tf_op jit(solution)/shard_map/all_gather | solution.py:892
  91.6 1.0 copy-done.6
  92.6 2.2 copy-done.7
  94.8 5.3 project.1
  100.1 1.0 copy-done.8
  101.0 1.0 copy-done.9
  102.0 1.0 copy-done.10
  103.0 84.0 %att_fwd.1 = (bf16[2048,256]{1,0:T(8,128)(2,1)}, f32[2048,128]{1,0:T(8,128)}, bf16[4,512,256]{2,1,0:T(8,128)(2,1)}, bf16[4,2,512,1024]{3,2,1,0:T(8,128)(2,1)}, b...) custom-call(s32[1]{0:T(128)} %copy.78.limit_ref, bf16[2048,256]{1,0:T(8,128)(2,1)} %copy-done.8, ...), custom_call_target="tpu_custom_call" | custom-call | flops 17179869184 | bytes 5242880 | tf_op jit(solution)/shard_map/att_fwd/pallas_call | solution.py:284
  187.0 1.8 fusion.35
  190.5 0.8 fusion.37
  192.1 1.4 add_convert_fusion.x_ref
  193.4 100.3 %ffn.1 = (bf16[4,512,1024]{2,1,0:T(8,128)(2,1)}, bf16[4,512,1024]{2,1,0:T(8,128)(2,1)}, bf16[4,3,128,1024]{3,2,1,0:T(8,128)(2,1)}) custom-call(bf16[512,1024]{1,0:T(8,128)(2,1)} %add_convert_fusion.x_ref, bf16[4,2,512,1024]{3,2,1,0:T(8,128)(2,1)} %get-tuple-element.40.gb_ref, bf16[3,512,1024]{2,1,0:T(8,128)(2,1)} %all-gather.8.cloned.1.call-done.w_ref), custom_call_target="tpu_custom_call" | custom-call | flops 38654705664 | bytes 31457280 | tf_op jit(solution)/shard_map/ffn/pallas_call | solution.py:823
  293.8 3.0 fusion.32
  296.8 1.0 fusion.8
  298.1 2.2 fusion.33
  302.1 1.6 maximum_bitcast_fusion
  303.8 40.7 %reduce-scatter.3.cloned.1.call-done = bf16[1,4,32,1024]{3,2,1,0:T(8,128)(2,1)} async-done(((bf16[8,4,32,1024]{3,2,1,0:T(8,128)(2,1)}), bf16[1,4,32,1024]{3,2,1,0:T(8,128)(2,1)}) %reduce-scatter.3.cloned.1.call-update) | async-done | bytes 262160 | tf_op jit(solution)/shard_map/reduce_scatter | solution.py:938
  344.4 4.1 pad_maximum_fusion
  349.2 63.6 %reduce-scatter.5.cloned.1.call-done = bf16[1,416,1024]{2,1,0:T(8,128)(2,1)} async-done(((bf16[4,416,1024]{2,1,0:T(8,128)(2,1)}), bf16[1,416,1024]{2,1,0:T(8,128)(2,1)}) %reduce-scatter.5.cloned.1.call-update) | async-done | bytes 851984 | tf_op jit(solution)/shard_map/reduce_scatter | solution.py:940
  413.4 198.2 %att_bwd.1 = (bf16[2048,768]{1,0:T(8,128)(2,1)}, bf16[4,512,768]{2,1,0:T(8,128)(2,1)}, bf16[3,512,1024]{2,1,0:T(8,128)(2,1)}) custom-call(s32[1]{0:T(128)} %copy.78.limit_ref, bf16[512,1024]{1,0:T(8,128)(2,1)} %copy-done.11, bf16[4,256,1024]{2,1,0:T(8,128)(2,1)} %bitcast.113, bf16[4,512,1024]{2,1,0:T(8,128)(2,1)} %get-tuple-element.41.parts_ref, ...), custom_call_target="tpu_custom_call" | custom-call | flops 42949672960 | bytes 10485760 | tf_op jit(solution)/shard_map/att_bwd/pallas_call | solution.py:469
  611.6 3.8 fusion.7
  615.4 51.7 %finish.1 = (f32[512,1024]{1,0:T(8,128)}, f32[1024,256]{1,0:T(8,128)}, f32[1024,256]{1,0:T(8,128)}, f32[1024,256]{1,0:T(8,128)}, f32[8,1024]{1,0:T(8,128)}) custom-call(bf16[2048,1024]{1,0:T(8,128)(2,1)} %all-gather.6.cloned.1.call-done.x_ref, bf16[2048,768]{1,0:T(8,128)(2,1)} %get-tuple-element.46.pk_ref, bf16[4,512,768]{2,1,0:T(8,128)(2,1)} %get-tuple-element.47.own_ref, ...), custom_call_target="tpu_custom_call" | custom-call | flops 6442450944 | bytes 20971520 | tf_op jit(solution)/shard_map/finish/pallas_call | solution.py:652
  667.1 1.6 fusion.36
  668.7 8.3 %all-gather.10.cloned.1.call-done = bf16[8,416,1024]{2,1,0:T(8,128)(2,1)} async-done(((bf16[1,416,1024]{2,1,0:T(8,128)(2,1)}), bf16[8,416,1024]{2,1,0:T(8,128)(2,1)}) %all-gather.10.cloned.1.call-update) | async-done | bytes 6815760 | tf_op jit(solution)/shard_map/all_gather | solution.py:941
  677.0 1.1 slice.92
  678.1 1.1 bitcast_convert_fusion.3
  679.2 5.2 fusion.34
  684.5 2.6 bitcast_convert_fusion.2
  687.1 5.3 copy.70
  692.4 4.1 bitcast_convert_fusion.1
  696.5 5.3 copy.71
  701.8 2.6 bitcast_convert_fusion
  704.4 1.3 copy.79
  706.4 1.0 copy.80
  708.0 1.0 copy.81
  709.0 1.0 copy.82
  (82 shorter events, 8.0 us)
Async XLA Ops:
  7.2 7.0 copy-start
  7.2 3.3 copy-start.12
  7.2 3.3 copy-start.22
  7.2 3.3 copy-start.24
  7.2 84.3 %all-gather.6.cloned.1.call-start = ((), (), s32[]{:S(2)}) async-start(), calls=%async_computation.2 | async-start | bytes 5242880 | tf_op jit(solution)/shard_map/all_gather | solution.py:892
  12.0 181.5 %all-gather.8.cloned.1.call-start = ((), (), s32[]{:S(2)}) async-start(), calls=%async_computation.3 | async-start | bytes 3932160 | tf_op jit(solution)/shard_map/all_gather | solution.py:910
  14.1 4.8 copy-start.5
  14.2 5.0 copy-start.4
  16.2 328.2 %reduce-scatter.3.cloned.1.call-start = ((), (), s32[]{:S(2)}) async-start(), calls=%async_computation.4 | async-start | bytes 2359296 | tf_op jit(solution)/shard_map/reduce_scatter | solution.py:938
  24.5 67.1 %copy-start.2 = (f32[2048,128]{1,0:T(8,128)}, f32[2048,128]{1,0:T(8,128)S(1)}, u32[]{:S(2)}) copy-start(f32[2048,128]{1,0:T(8,128)S(1)} %get-tuple-element.73.sin_ref) | copy-start | bytes 3145732
  24.5 67.1 %copy-start.3 = (f32[2048,128]{1,0:T(8,128)}, f32[2048,128]{1,0:T(8,128)S(1)}, u32[]{:S(2)}) copy-start(f32[2048,128]{1,0:T(8,128)S(1)} %get-tuple-element.74.cos_ref) | copy-start | bytes 3145732
  91.5 1.0 copy-start.6
  92.6 2.2 copy-start.7
  100.1 1.0 copy-start.8
  101.0 1.0 copy-start.9
  102.0 1.0 copy-start.10
  187.0 1.9 copy-start.15
  189.3 1.2 copy-start.13
  191.4 0.7 copy-start.21
  191.4 0.7 copy-start.23
  296.8 1.2 copy-start.14
  298.0 2.2 copy-start.16
  300.2 1.4 copy-start.11
  303.7 109.0 %reduce-scatter.5.cloned.1.call-start = ((), (), s32[]{:S(2)}) async-start(), calls=%async_computation.5 | async-start | bytes 4259840 | tf_op jit(solution)/shard_map/reduce_scatter | solution.py:940
  348.5 266.9 %all-gather.12.cloned.1.call-start = ((), (), s32[]{:S(2)}) async-start(), calls=%async_computation.7 | async-start | bytes 7864320 | tf_op jit(solution)/shard_map/all_gather | solution.py:928
  349.1 327.9 %all-gather.10.cloned.1.call-start = ((), (), s32[]{:S(2)}) async-start(), calls=%async_computation.6 | async-start | bytes 7667712 | tf_op jit(solution)/shard_map/all_gather | solution.py:941
  701.8 2.6 copy-start.17
  704.4 2.0 copy-start.20
  706.4 1.6 copy-start.19
  706.4 2.6 copy-start.18
  706.4 3.5 copy-start.1
Sparse Core Ops, SparseCore 0:
  12.1 79.3 all-gather.5
  93.7 88.7 all-gather.7
  303.8 40.5 reduce-scatter.2
  348.6 64.0 reduce-scatter.4
  414.8 196.7 all-gather.11
  613.5 63.4 all-gather.9

commit v2 on v1

--- a/solution.py
+++ b/solution.py
@@ -9,9 +9,7 @@
 from jax.sharding import PartitionSpec as P
 
 HD = 64
-WIDE = 256
 EPS = 1e-05
-LOG2E = math.log2(math.e)
 SCALE = 1.0 / math.sqrt(HD)
 F32 = jnp.float32
 BF = jnp.bfloat16
@@ -50,53 +48,60 @@
     return jnp.cos(angles), jnp.sin(angles) * sign[None, :]
 
 
-def project_kernel(width, x_ref, wq_ref, wk_ref, wv_ref, cos_ref, sin_ref, q_ref, k_ref, v_ref):
+def project_kernel(
+    limit_ref, x_ref, wq_ref, wk_ref, wv_ref, cos_ref, sin_ref, q_ref, k_ref, v_ref
+):
     x = x_ref[...]
-    cosine = jnp.tile(cos_ref[...], (1, width // (2 * HD)))
-    sine = jnp.tile(sin_ref[...], (1, width // (2 * HD)))
-    for w_ref, out_ref in ((wq_ref, q_ref), (wk_ref, k_ref)):
+    block = x.shape[0]
+    heads = q_ref.shape[0]
+    width = heads * HD
+    cosine = jnp.tile(cos_ref[...], (1, heads // 2))
+    sine = jnp.tile(sin_ref[...], (1, heads // 2))
+    lane = lanes((block, 128))
+    row = pl.program_id(0) * block + lax.broadcasted_iota(jnp.int32, (block, 128), 0)
+    ones = jnp.where(lane < HD + 3, 1.0, 0.0)
+    bias = jnp.where(lane == HD + 3, jnp.where(row < limit_ref[0], 0.0, -1e30), ones)
+    unit = jnp.where(lane == HD + 3, 1.0, 0.0)
+
+    def turned(w_ref):
         raw = dot(x, w_ref[...])
-        out_ref[...] = (raw * cosine + partner(raw) * sine).astype(BF)
-    v_ref[...] = dot(x, wv_ref[...]).astype(BF)
-
-
-def project(rows, w_query, w_key, w_value, cosine, sine, block=512):
+        return raw * cosine + partner(raw) * sine
+
+    def put(out_ref, values, extra):
+        for h in range(heads):
+            own = values[:, h // 2 * 128 : h // 2 * 128 + 128]
+            own = pltpu.roll(own, HD, 1) if h % 2 else own
+            out_ref[h] = jnp.where(lane < HD, own, extra).astype(BF)
+
+    put(q_ref, turned(wq_ref).astype(BF).astype(F32) * SCALE, unit)
+    put(k_ref, turned(wk_ref), bias)
+    put(v_ref, dot(x, wv_ref[...]), ones)
+
+
+def project(rows, w_query, w_key, w_value, cosine, sine, limit, block=512):
     n, depth = rows.shape
     width = w_query.shape[1]
-    whole = pl.BlockSpec((depth, width), lambda i: (0, 0))
-    table = pl.BlockSpec((block, 2 * HD), lambda i: (i, 0))
-    out = pl.BlockSpec((block, width), lambda i: (i, 0))
+    heads = width // HD
+    whole = pl.BlockSpec((depth, width), lambda i, *_: (0, 0))
+    table = pl.BlockSpec((block, 2 * HD), lambda i, *_: (i, 0))
+    out = pl.BlockSpec((heads, block, 128), lambda i, *_: (0, i, 0))
     return pl.pallas_call(
-        functools.partial(project_kernel, width),
-        out_shape=(jax.ShapeDtypeStruct((n, width), BF),) * 3,
-        grid=(n // block,),
-        in_specs=[pl.BlockSpec((block, depth), lambda i: (i, 0)), whole, whole, whole, table, table],
-        out_specs=(out, out, out),
+        project_kernel,
+        out_shape=(jax.ShapeDtypeStruct((heads, n, 128), BF),) * 3,
+        grid_spec=pltpu.PrefetchScalarGridSpec(
+            num_scalar_prefetch=1,
+            grid=(n // block,),
+            in_specs=[pl.BlockSpec((block, depth), lambda i, *_: (i, 0))]
+            + [whole] * 3
+            + [table] * 2,
+            out_specs=(out, out, out),
+        ),
         compiler_params=pltpu.CompilerParams(vmem_limit_bytes=40 << 20),
         cost_estimate=pl.CostEstimate(
-            flops=2 * n * depth * 3 * width, bytes_accessed=2 * (n * depth + 3 * n * width), transcendentals=0
+            flops=2 * n * depth * 3 * width, bytes_accessed=2 * (n * depth + 6 * n * width), transcendentals=0
         ),
         name="project",
-    )(rows, w_query, w_key, w_value, cosine, sine)
-
-
-def own_lanes(h, shape):
-    lane = lanes(shape)
-    off = lax.rem(lane - h * HD + shape[1], shape[1])
-    return off < HD, off
-
-
-def attend(q, k, v):
-    scores = dot(q, k, NT)
-    peak = jnp.max(scores, axis=1, keepdims=True)
-    return dot(jnp.exp2(scores - peak).astype(BF), v), peak
-
-
-def query_operand(h, q):
-    own, off = own_lanes(h, q.shape)
-    q = jnp.where(own, q.astype(F32), 0.0) * (LOG2E * SCALE)
-    high = q.astype(BF).astype(F32)
-    return high + pltpu.roll(q - high, HD, 1), own, off - 2 * HD
+    )(limit, rows, w_query, w_key, w_value, cosine, sine)
 
 
 def differ(a, b, bits):
@@ -137,19 +142,18 @@
 
 
 def att_fwd_kernel(
-    n, chips, limit_ref, q_ref, k_ref, v_ref, gb_ref, wo_ref,
-    ctx_ref, lse_ref, out_ref, gb_all, wo_z, wo_all, ka, va, send_sem, recv_sem, own_sem,
+    n, chips, q_ref, k_ref, v_ref, gb_ref, wo_ref,
+    ctx_ref, lse_ref, out_ref, gb_all, wo_z, wo_all, send_sem, recv_sem, own_sem,
     gs_send, gs_recv, gr_send, gr_recv, wz_send, wz_recv, ws_send, ws_recv, wr_send, wr_recv, keep_sem,
 ):
     s = pl.program_id(0)
     h = pl.program_id(1)
     heads = pl.num_programs(1)
-    rows = q_ref.shape[0] // n
+    rows = q_ref.shape[1] // n
     me = lax.axis_index("tensor")
     place = lax.axis_index("dp")
     core = lax.rem(place, 2)
     bits = chips.bit_length() - 1
-    limit = limit_ref[0]
 
     def spread_gb(c):
         return remote(
@@ -218,26 +222,19 @@
             spread_gb(c).wait_recv()
             relay_gb(c).start()
 
-    @pl.when(s == 0)
-    def _():
-        own, off = own_lanes(h, k_ref.shape)
-        k = jnp.where(own, k_ref[...].astype(F32), 0.0)
-        row = lax.broadcasted_iota(jnp.int32, k.shape, 0)
-        bias = jnp.where(row < limit, 0.0, -1e30)
-        ka[h] = jnp.where(off == 2 * HD, bias, k + pltpu.roll(k, HD, 1)).astype(BF)
-        v = jnp.where(own, v_ref[...].astype(F32), 0.0)
-        va[h] = jnp.where(off == HD, 1.0, v).astype(BF)
-
     owner = ring(n, s + 1)
     block = pl.ds(pl.multiple_of(owner * rows, rows), rows)
-    q, own, off = query_operand(h, q_ref[block, :])
-    acc, peak = attend(jnp.where(off == 0, 1.0, q).astype(BF), ka[h], va[h])
-    total = jnp.sum(jnp.where(off == -HD, acc, 0.0), axis=1, keepdims=True)
-    out = (acc * (1.0 / total)).astype(BF)
-    ctx_ref[block, :] = jnp.where(own, out, ctx_ref[block, :])
-    lse_ref[block, :] = jnp.where(
-        lanes((rows, 128)) == h, peak + jnp.log2(total), lse_ref[block, :]
-    )
+    scores = dot(q_ref[h, block, :], k_ref[h], NT)
+    peak = jnp.max(scores, axis=1, keepdims=True)
+    acc = dot(jnp.exp(scores - peak).astype(BF), v_ref[h])
+    lane = lanes((rows, 128))
+    total = jnp.sum(jnp.where(lane == HD, acc, 0.0), axis=1, keepdims=True)
+    out = acc * (1.0 / total)
+    odd = lax.rem(h, 2)
+    out = jnp.where(odd == 1, pltpu.roll(out, HD, 1), out).astype(BF)
+    pair = pl.ds(pl.multiple_of(h // 2 * 128, 128), 128)
+    ctx_ref[block, pair] = jnp.where((lane >= HD) == (odd == 1), out, ctx_ref[block, pair])
+    lse_ref[block, :] = jnp.where(lane == h, peak + jnp.log(total), lse_ref[block, :])
 
     def push(step):
         return pltpu.make_async_remote_copy(
@@ -270,16 +267,17 @@
                 spread_wo(c).wait_send()
 
 
-def att_fwd(q, k, v, grad_rows, w_out_piece, limit, heads, n, devices):
-    total, width = q.shape
+def att_fwd(q, k, v, grad_rows, w_out_piece, n, devices):
+    heads, total, _ = q.shape
+    width = heads * HD
     rows = total // n
     depth = grad_rows.shape[1]
     share = w_out_piece.shape[0]
     chips = devices // 2
     hbm = pl.BlockSpec(memory_space=pl.ANY)
 
-    def whole(d):
-        return pl.BlockSpec((total, d), lambda *_: (0, 0), pipeline_mode=pl.Buffered(1))
+    def whole(*shape):
+        return pl.BlockSpec(shape, lambda *_: (0,) * len(shape), pipeline_mode=pl.Buffered(1))
 
     return pl.pallas_call(
         functools.partial(att_fwd_kernel, n, chips),
@@ -292,12 +290,11 @@
             jax.ShapeDtypeStruct((n, devices, share, depth), BF),
         ),
         grid_spec=pltpu.PrefetchScalarGridSpec(
-            num_scalar_prefetch=1,
+            num_scalar_prefetch=0,
             grid=(n, heads),
-            in_specs=[whole(width)] * 3 + [hbm] * 2,
-            out_specs=[whole(width), whole(128)] + [hbm] * 4,
-            scratch_shapes=[pltpu.VMEM((heads, total, width), BF)] * 2
-            + [pltpu.SemaphoreType.DMA((n - 1,))] * 2
+            in_specs=[whole(heads, total, 128)] * 3 + [hbm] * 2,
+            out_specs=[whole(total, width), whole(total, 128)] + [hbm] * 4,
+            scratch_shapes=[pltpu.SemaphoreType.DMA((n - 1,))] * 2
             + [pltpu.SemaphoreType.DMA]
             + [pltpu.SemaphoreType.DMA((chips,))] * 4
             + [pltpu.SemaphoreType.DMA((n - 1,))] * 2
@@ -305,7 +302,7 @@
             + [pltpu.SemaphoreType.DMA((3,))],
         ),
         compiler_params=pltpu.CompilerParams(
-            vmem_limit_bytes=56 << 20, collective_id=1, has_side_effects=True
+            vmem_limit_bytes=40 << 20, collective_id=1, has_side_effects=True
         ),
         cost_estimate=pl.CostEstimate(
             flops=4 * total * total * 256 * heads,
@@ -313,22 +310,26 @@
             transcendentals=total * total * heads,
         ),
         name="att_fwd",
-    )(limit, q, k, v, grad_rows, w_out_piece)
+    )(q, k, v, grad_rows, w_out_piece)
 
 
 def att_bwd_kernel(
-    n, bk, chips, heads, limit_ref, ga_ref, wo_ref, parts_ref, q_ref, k_ref, v_ref, ctx_ref, lse_ref,
-    cos_ref, sin_ref, pk_ref, own_ref, sums_ref, do, gc, ka, va, dka, dva, dqs, dvs,
+    n, bk, chips, ga_ref, wo_ref, cown_ref, parts_ref, q_ref, k_ref, v_ref, ctx_ref, lse_ref,
+    cos_ref, sin_ref, pk_ref, own_ref, sums_ref, og_ref, do, gc, dka, dva, dqs, dvs,
+    og_full, og_own, og_mate, og_sib, og_land, og_piece, og_z,
     send_sem, recv_sem, out_send, out_recv, pk_send, pk_recv, keep_sem,
+    om_send, om_recv, op_send, op_recv, oz_send, oz_recv,
 ):
     h = pl.program_id(0)
     t = pl.program_id(1)
-    total, width = k_ref.shape
+    heads, total, _ = k_ref.shape
     rows = total // n
     me = lax.axis_index("tensor")
-    limit = limit_ref[0]
+    place = lax.axis_index("dp")
+    core = lax.rem(place, 2)
+    bits = chips.bit_length() - 1
+    share = og_ref.shape[0]
     mine = pl.ds(pl.multiple_of(me * rows, rows), rows)
-    to_first = lax.rem(width - h * HD, width)
 
     def push(step):
         return remote(
@@ -364,7 +365,7 @@
 
     @pl.when((h == 0) & (t == 0))
     def _():
-        greet(n, chips)
+        greet(n, chips, True)
         for s in range(1, chips):
             push_out(s).start()
 
@@ -376,71 +377,109 @@
         lax.fori_loop(0, n - 1, send, 0)
         do[mine, :] = dot(ga_ref[...], wo_ref[me], NT).astype(BF)
 
+    def og_swap():
+        return remote(og_mate, og_sib, om_send, om_recv, dp=sibling())
+
+    def og_push(s):
+        return remote(og_sib.at[s], og_land.at[s], op_send.at[s], op_recv.at[s], dp=same_core(s, chips))
+
+    def og_over(step):
+        to = ring(n, step + 1)
+        return remote(og_piece.at[to], og_z.at[me], oz_send.at[step], oz_recv.at[step], tensor=to)
+
+    @pl.when((h == 0) & (t == 1))
+    def _():
+        def term(part, carry):
+            og_full[...] = dot(cown_ref[part], ga_ref[...], TN)
+            for s in range(chips):
+                start = differ(place // 2, s, bits) * 2
+                here = pl.ds(pl.multiple_of((start + core) * share, share), share)
+                there = pl.ds(pl.multiple_of((start + 1 - core) * share, share), share)
+                og_own[s, part] = og_full[here, :]
+                og_mate[s, part] = og_full[there, :].astype(BF)
+            return carry
+
+        lax.fori_loop(0, n, term, 0)
+        og_swap().start()
+
+    @pl.when((h == 0) & (t == n - 1))
+    def _():
+        og_swap().wait_recv()
+        for s in range(chips):
+            og_sib[s] = (og_own[s] + og_sib[s].astype(F32)).astype(BF)
+            if s:
+                og_push(s).start()
+
+    @pl.when((h == 1) & (t == 1))
+    def _():
+        joined = og_sib[0].astype(F32)
+        for s in range(1, chips):
+            og_push(s).wait_recv()
+            joined = joined + og_land[s].astype(F32)
+        og_piece[...] = joined.astype(BF)
+        for step in range(n - 1):
+            og_over(step).start()
+
+    @pl.when((h == heads - 1) & (t == n - 1))
+    def _():
+        og_z[me] = og_piece[me]
+        for step in range(n - 1):
+            og_over(step).wait_recv()
+        joined = og_z[0].astype(F32)
+        for part in range(1, n):
+            joined = joined + og_z[part].astype(F32)
+        og_ref[...] = joined.astype(BF)
+
     @pl.when((h == 0) & (t > 0))
     def _():
         push(t - 1).wait_recv()
 
     @pl.when(t == 0)
     def _():
-        lane = lanes((total, width))
-        row = lax.broadcasted_iota(jnp.int32, (total, width), 0)
-        k = jnp.where(lane < HD, pltpu.roll(k_ref[...].astype(F32), to_first, 1), 0.0)
-        k = jnp.where(
-            lane == 2 * HD + 3, jnp.where(row < limit, 0.0, -1e30), k + pltpu.roll(k, HD, 1)
-        )
-        ones = (lane >= 2 * HD) & (lane < 2 * HD + 3)
-        ka[...] = jnp.where(ones, 1.0, k).astype(BF)
-        v = jnp.where(lane < HD, pltpu.roll(v_ref[...].astype(F32), to_first, 1), 0.0)
-        va[...] = jnp.where(ones, 1.0, v).astype(BF)
         dka[...] = jnp.zeros_like(dka)
         dva[...] = jnp.zeros_like(dva)
 
     source = ring(n, n - t)
     block = pl.ds(pl.multiple_of(source * rows, rows), rows)
-    off = lanes((rows, width)) - 2 * HD
-    q = pltpu.roll(q_ref[block, :].astype(F32), to_first, 1) * (LOG2E * SCALE)
-    q = jnp.where(off < -HD, q, 0.0)
-    high = q.astype(BF).astype(F32)
-    q = high + pltpu.roll(q - high, HD, 1)
-    logsum = jnp.sum(
-        jnp.where(lanes((rows, 128)) == h, lse_ref[block, :], 0.0), axis=1, keepdims=True
-    )
+    pair = columns(h // 2)
+    odd = lax.rem(h, 2) == 1
+    lane = lanes((rows, 128))
+    off = lane - HD
+    logsum = jnp.sum(jnp.where(lane == h, lse_ref[block, :], 0.0), axis=1, keepdims=True)
     a, b, c = split3(-logsum)
-    q = jnp.where(off == 0, a, jnp.where(off == 1, b, jnp.where(off == 2, c, q)))
-    q = jnp.where(off == 3, 1.0, q).astype(BF)
-    g = jnp.where(off < -HD, pltpu.roll(do[block, :].astype(F32), to_first, 1), 0.0)
-    delta = jnp.sum(
-        g * pltpu.roll(ctx_ref[block, :].astype(F32), to_first, 1), axis=1, keepdims=True
-    )
+    q = q_ref[h, block, :].astype(F32)
+    q = jnp.where(off == 0, a, jnp.where(off == 1, b, jnp.where(off == 2, c, q))).astype(BF)
+    g = jnp.where((lane >= HD) == odd, do[block, pair].astype(F32), 0.0)
+    delta = jnp.sum(g * ctx_ref[block, pair].astype(F32), axis=1, keepdims=True)
     a, b, c = split3(-delta)
+    g = jnp.where(odd, pltpu.roll(g, HD, 1), g)
     g = jnp.where(off == 0, a, jnp.where(off == 1, b, jnp.where(off == 2, c, g))).astype(BF)
-    acc = jnp.zeros((rows, width), F32)
+    acc = jnp.zeros((rows, 128), F32)
     for j in range(total // bk):
         rk = pl.ds(j * bk, bk)
-        kt = ka[rk, :]
-        probs = jnp.exp2(dot(kt, q, NT))
-        grad = (probs * dot(va[rk, :], g, NT)).astype(BF)
+        kt = k_ref[h, rk, :]
+        probs = jnp.exp(dot(kt, q, NT))
+        grad = (probs * dot(v_ref[h, rk, :], g, NT)).astype(BF)
         dva[rk, :] += dot(probs.astype(BF), g)
         dka[rk, :] += dot(grad, q)
         acc = acc + dot(grad, kt, TN)
-    dqs[block, :] = acc[:, :128] * SCALE
+    dqs[block, :] = acc * SCALE
 
     @pl.when(t == n - 1)
     def _():
         first = lanes((total, 128)) < HD
-        dk = dka[:, :128]
-        grad = jnp.where(first, dqs[...], (dk + pltpu.roll(dk, HD, 1)) * (1.0 / LOG2E))
+        grad = jnp.where(first, dqs[...], pltpu.roll(dka[...], HD, 1))
         grad = grad * cos_ref[...] - partner(grad) * sin_ref[...]
         pk_ref[:, columns(h)] = grad.astype(BF)
         send_pack(h)
 
         @pl.when(lax.rem(h, 2) == 0)
         def _():
-            dvs[...] = dva[:, :128]
+            dvs[...] = dva[...]
 
         @pl.when(lax.rem(h, 2) == 1)
         def _():
-            both = jnp.where(first, dvs[...], pltpu.roll(dva[:, :128], HD, 1))
+            both = jnp.where(first, dvs[...], pltpu.roll(dva[...], HD, 1))
             pk_ref[:, columns(heads + h // 2)] = both.astype(BF)
             send_pack(heads + h // 2)
 
@@ -450,16 +489,23 @@
             push(step).wait_send()
         for s in range(1, chips):
             push_out(s).wait()
+        og_swap().wait_send()
+        for s in range(1, chips):
+            og_push(s).wait_send()
+        for step in range(n - 1):
+            og_over(step).wait_send()
         for slot in range(heads + heads // 2):
             keep(slot).wait()
             for step in range(n - 1):
                 push_pack(slot, step).wait()
 
 
-def att_bwd(grad_attn, w_out, parts, q, k, v, ctx, lse, limit, cosine, sine, heads, n, bk=512):
-    total, width = q.shape
+def att_bwd(grad_attn, w_out, ctx_own, parts, q, k, v, ctx, lse, cosine, sine, n, bk=512):
+    heads, total, _ = q.shape
+    width = heads * HD
     rows, depth = grad_attn.shape
     chips = parts.shape[0]
+    share = width // (2 * chips)
     slots = heads + heads // 2
     hbm = pl.BlockSpec(memory_space=pl.ANY)
 
@@ -467,33 +513,42 @@
         return pl.BlockSpec(shape, lambda *_: (0,) * len(shape), pipeline_mode=pl.Buffered(1))
 
     return pl.pallas_call(
-        functools.partial(att_bwd_kernel, n, bk, chips, heads),
+        functools.partial(att_bwd_kernel, n, bk, chips),
         out_shape=(
             jax.ShapeDtypeStruct((total, slots * 128), BF),
             jax.ShapeDtypeStruct((n, rows, slots * 128), BF),
             jax.ShapeDtypeStruct((chips - 1, rows, depth), BF),
+            jax.ShapeDtypeStruct((share, depth), BF),
         ),
         grid_spec=pltpu.PrefetchScalarGridSpec(
-            num_scalar_prefetch=1,
+            num_scalar_prefetch=0,
             grid=(heads, n),
-            in_specs=[whole(rows, depth), whole(n, width, depth), hbm]
-            + [whole(total, width)] * 4
+            in_specs=[whole(rows, depth), whole(n, width, depth), whole(n, rows, width), hbm]
+            + [whole(heads, total, 128)] * 3
+            + [whole(total, width)]
             + [whole(total, 128)] * 3,
-            out_specs=[whole(total, slots * 128), hbm, hbm],
+            out_specs=[whole(total, slots * 128), hbm, hbm, whole(share, depth)],
             scratch_shapes=[
                 pltpu.VMEM((total, width), BF),
                 pltpu.VMEM((n - 1, rows, width), BF),
-                pltpu.VMEM((total, width), BF),
-                pltpu.VMEM((total, width), BF),
-                pltpu.VMEM((total, width), F32),
-                pltpu.VMEM((total, width), F32),
-                pltpu.VMEM((total, 128), F32),
-                pltpu.VMEM((total, 128), F32),
+            ]
+            + [pltpu.VMEM((total, 128), F32)] * 4
+            + [
+                pltpu.VMEM((width, depth), F32),
+                pltpu.VMEM((chips, n, share, depth), F32),
+                pltpu.VMEM((chips, n, share, depth), BF),
+                pltpu.VMEM((chips, n, share, depth), BF),
+                pltpu.VMEM((chips, n, share, depth), BF),
+                pltpu.VMEM((n, share, depth), BF),
+                pltpu.VMEM((n, share, depth), BF),
             ]
             + [pltpu.SemaphoreType.DMA((n - 1,))] * 2
             + [pltpu.SemaphoreType.DMA((chips - 1,))] * 2
             + [pltpu.SemaphoreType.DMA((slots, n - 1))] * 2
-            + [pltpu.SemaphoreType.DMA((slots,))],
+            + [pltpu.SemaphoreType.DMA((slots,))]
+            + [pltpu.SemaphoreType.DMA] * 2
+            + [pltpu.SemaphoreType.DMA((chips,))] * 2
+            + [pltpu.SemaphoreType.DMA((n - 1,))] * 2,
         ),
         compiler_params=pltpu.CompilerParams(
             vmem_limit_bytes=56 << 20, collective_id=2, has_side_effects=True
@@ -504,7 +559,7 @@
             transcendentals=total * total * heads,
         ),
         name="att_bwd",
-    )(limit, grad_attn, w_out, parts, q, k, v, ctx, lse, cosine, sine)
+    )(grad_attn, w_out, ctx_own, parts, q, k, v, ctx, lse, cosine, sine)
 
 
 def finish_kernel(
@@ -884,15 +939,11 @@
     local_rows, depth = tokens.shape
     length = local_rows * n
     width = w_query.shape[1]
-    heads = width // HD
     row_ids = lax.axis_index("tensor") * local_rows + lax.iota(jnp.int32, local_rows)
     valid = (row_ids < lengths[0])[:, None]
 
     def gather(x):
         return lax.all_gather(x, "tensor", axis=0, tiled=True)
-
-    def padded(x):
-        return x if width >= WIDE else jnp.pad(x, ((0, 0), (0, WIDE - width)))
 
     inputs = tokens.astype(F32)
     scaled1, _ = norm_parts(inputs)
@@ -908,16 +959,13 @@
 
     weights = jnp.stack([piece(w_gate, 1).T, piece(w_up, 1).T, piece(down_weight, 0)])
     weights = lax.all_gather(weights, "tensor", axis=1, tiled=True)
-    q, k, v = project(attn_rows, w_query, w_key, w_value, cosine, sine)
-    q, k, v = padded(q), padded(k), padded(v)
+    q, k, v = project(attn_rows, w_query, w_key, w_value, cosine, sine, lengths)
     context, logsum, context_own, grad_branch, _, w_out_all = att_fwd(
         q, k, v, grad_out.astype(BF),
         lax.dynamic_slice_in_dim(w_out, place * (width // devices), width // devices, 0),
-        lengths, heads, n, devices,
+        n, devices,
     )
     w_out_all = w_out_all.reshape(n, width, depth)
-    if width < WIDE:
-        w_out_all = jnp.pad(w_out_all, ((0, 0), (0, WIDE - width), (0, 0)))
     attn_out = sum(dot(context_own[t], w_out_all[t]).astype(BF).astype(F32) for t in range(n))
     middle = inputs + attn_out
     scaled2, inverse2 = norm_parts(middle)
@@ -933,21 +981,20 @@
     )
     grad_middle = grad_out + grad_norm2
     grad_attn = grad_middle.astype(BF)
-    parts = jnp.stack([dot(context_own[t, :, :width], grad_attn, TN).astype(BF) for t in range(n)])
-    parts = parts.reshape(n, devices, width // devices, depth).transpose(1, 0, 2, 3)
-    parts = lax.psum_scatter(parts, "dp", scatter_dimension=0, tiled=True)[0]
-    grads = jnp.concatenate([ffn_grads.reshape(n, 3 * share, depth), parts], axis=1)
-    grads = lax.psum_scatter(grads, "tensor", scatter_dimension=0, tiled=True)[0]
-    grads = lax.all_gather(grads, "dp", axis=0)
+    ffn_grads = ffn_grads.reshape(n, 3 * share, depth)
+    ffn_grads = lax.psum_scatter(ffn_grads, "tensor", scatter_dimension=0, tiled=True)[0]
+    w_packed, grad_attn = lax.optimization_barrier((w_packed, grad_attn))
+    packed, packed_own, out_sums, out_piece = att_bwd(
+        grad_attn, w_out_all, context_own, out_parts, q, k, v, context, logsum, cosine, sine, n
+    )
+    ffn_grads, out_piece = lax.optimization_barrier((ffn_grads, out_piece))
+    grads = lax.all_gather(jnp.concatenate([ffn_grads, out_piece]), "dp", axis=0)
     gate_grad, up_grad, down_grad = (
         grads[:, k * share : (k + 1) * share].reshape(devices * share, depth).astype(F32)
         for k in range(3)
     )
     gate_grad, up_grad = gate_grad.T, up_grad.T
     out_grad = grads[:, 3 * share :].reshape(width, depth).astype(F32)
-    packed, packed_own, out_sums = att_bwd(
-        grad_attn, w_out_all, out_parts, q, k, v, context, logsum, lengths, cosine, sine, heads, n
-    )
     ffn_out = sum(x.astype(F32) for x in (out_parts[0], *out_sums))
     output = jnp.where(valid, middle + ffn_out, 0.0).astype(BF)
     input_grad, query_grad, key_grad, value_grad, sums = finish(

time: 725 us -> 567 us (0.78)
  waiting for transfers between devices: 174 us -> 68.9 us
  Pallas kernels: 440 us -> 400 us
  other arithmetic: 44.2 us -> 36.7 us
    reduce_scatter x2 -> x1, waiting for transfers between devices: 104 us -> 0.02 us  [on_device(): lax.psum_scatter(ffn_grads, 'tensor', scatter_dimension=0, tiled=True)[0]]
    pallas_call x2, Pallas kernels: 203 us -> 166 us  [the longest x1 160 us: att_bwd(): pl.pallas_call(functools.partial(att_bwd_kernel, n, bk, chips), out_shape...]
    pallas_call x1, Pallas kernels: 84 us -> 72.3 us  [att_fwd(): pl.pallas_call(functools.partial(att_fwd_kernel, n, chips), out_shape=(ja...]
    all_gather x1, waiting for transfers between devices: 8.31 us -> 0.21 us  [on_device(): lax.all_gather(jnp.concatenate([ffn_grads, out_piece]), 'dp', axis=0)]
    unnamed x59 -> x69, local copies, waits for them, and re-layouts: 16.1 us -> 16.6 us
  transfers between devices with their start and end apart: 6 -> 5, of which waited for: 4 -> 3; matrix products, arithmetic and copies ran while one was open for 4% -> 5% of each run, Pallas kernels for 47% -> 72%
where the time goes in v2:
time: 567 us; the launch traced here: 560 us
  Pallas kernels  400 us (71%)
  waiting for transfers between devices  68.9 us (12%)
  other arithmetic  36.7 us (6%)
  local copies, waits for them, and re-layouts  36.2 us (6%)
  between operations  15.1 us (3%)
    pallas_call x1, Pallas kernels, att_bwd(): pl.pallas_call(functools.partial(att_bwd_kernel, n, bk, chips), out_shape...  160 us
    pallas_call x1, Pallas kernels, ffn(): pl.pallas_call(functools.partial(ffn_kernel, chips), out_shape=(jax.Shape...  106 us
    pallas_call x1, Pallas kernels, att_fwd(): pl.pallas_call(functools.partial(att_fwd_kernel, n, chips), out_shape=(ja...  72.3 us
    all_gather x1, waiting for transfers between devices, gather(): return lax.all_gather(x, 'tensor', axis=0, tiled=True)  64.7 us
    pallas_call x1, Pallas kernels, finish(): pl.pallas_call(functools.partial(finish_kernel, chips, n, width), out_sha...  56.1 us
    unnamed x69, local copies, waits for them, and re-layouts  16.6 us
  transfers between devices with their start and end apart: 5, of which 3 were waited for; matrix products, arithmetic and copies ran while one was open for 5% of the time, Pallas kernels for 72%

profile of v2, /device:TPU:9, one launch (start us, length us, event | category | flops | bytes accessed | tf_op | source)
XLA Modules:
  0.0 559.6 jit_solution(940002693014064429)
XLA Ops:
  7.3 1.6 convert_reduce_fusion
  8.9 1.6 fusion.2
  10.5 1.4 fusion.5
  12.0 1.1 constant_dynamic-slice_fusion
  13.3 0.9 copy.50
  14.2 2.0 pad_maximum_fusion.3
  17.5 0.8 copy-done.10
  18.6 0.9 constant_dynamic-slice_fusion.2.wo_ref
  19.4 1.3 pad_maximum_fusion
  20.7 3.9 sine_multiply_fusion
  24.6 2.2 fusion.9.gb_ref
  26.9 64.7 %all-gather.7.cloned.1.call-done.x_ref = bf16[2048,1024]{1,0:T(8,128)(2,1)} async-done(((bf16[512,1024]{1,0:T(8,128)(2,1)}), bf16[2048,1024]{1,0:T(8,128)(2,1)}) %all-gather.7.cloned.1.call-update) | async-done | bytes 4194320 | tf_op jit(solution)/shard_map/all_gather | solution.py:946
  91.5 1.0 copy-done.7
  92.6 1.0 copy-done.9
  93.6 1.0 copy-done.11
  94.7 2.2 copy-done.12
  96.9 6.0 %project.1 = (bf16[4,2048,128]{2,1,0:T(8,128)(2,1)S(1)}, bf16[4,2048,128]{2,1,0:T(8,128)(2,1)S(1)}, bf16[4,2048,128]{2,1,0:T(8,128)(2,1)S(1)}) custom-call(s32[1]{0:T(128)} %copy.56.limit_ref, bf16[2048,1024]{1,0:T(8,128)(2,1)S(1)} %copy-done.12, bf16[1024,256]{1,0:T(8,128)(2,1)S(1)} %copy-done.7, bf16[1024,256]{1,0:T(8,128)(2,1)S(1)} %copy-done.9, ...), custom_call_target="tpu_custom_call" | custom-call | flops 3221225472 | bytes 10485760 | tf_op jit(solution)/shard_map/project/pallas_call | solution.py:88
  102.9 72.3 %att_fwd.1 = (bf16[2048,256]{1,0:T(8,128)(2,1)S(1)}, f32[2048,128]{1,0:T(8,128)S(1)}, bf16[4,512,256]{2,1,0:T(8,128)(2,1)S(1)}, bf16[4,2,512,1024]{3,2,1,0:T(8,1...) custom-call(bf16[4,2048,128]{2,1,0:T(8,128)(2,1)S(1)} %get-tuple-element.39.q_ref, ...), custom_call_target="tpu_custom_call" | custom-call | flops 17179869184 | bytes 5242880 | tf_op jit(solution)/shard_map/att_fwd/pallas_call | solution.py:282
  175.3 1.0 copy-done.17
  176.5 1.1 copy-done.2
  178.4 0.4 convolution_convert_fusion.2
  179.6 0.8 fusion.29
  181.1 1.4 add_convert_fusion.x_ref
  182.6 106.1 %ffn.1 = (bf16[4,512,1024]{2,1,0:T(8,128)(2,1)}, bf16[4,512,1024]{2,1,0:T(8,128)(2,1)}, bf16[4,3,128,1024]{3,2,1,0:T(8,128)(2,1)}) custom-call(bf16[512,1024]{1,0:T(8,128)(2,1)} %add_convert_fusion.x_ref, bf16[4,2,512,1024]{3,2,1,0:T(8,128)(2,1)} %get-tuple-element.45.gb_ref, bf16[3,512,1024]{2,1,0:T(8,128)(2,1)} %all-gather.9.cloned.1.call-done.w_ref), custom_call_target="tpu_custom_call" | custom-call | flops 38654705664 | bytes 31457280 | tf_op jit(solution)/shard_map/ffn/pallas_call | solution.py:878
  288.7 3.0 fusion.24
  291.8 1.0 fusion.8
  293.0 2.3 fusion.25
  295.3 3.9 all-gather.11.cloned.1.call-done
  299.2 159.9 %att_bwd.1 = (bf16[2048,768]{1,0:T(8,128)(2,1)}, bf16[4,512,768]{2,1,0:T(8,128)(2,1)}, bf16[3,512,1024]{2,1,0:T(8,128)(2,1)}, bf16[32,1024]{1,0:T(8,128)(2,1)}) custom-call(bf16[512,1024]{1,0:T(8,128)(2,1)} %get-tuple-element.49.ga_ref, bf16[4,256,1024]{2,1,0:T(8,128)(2,1)} %bitcast.84, bf16[4,512,256]{2,1,0:T(8,128)(2,1)} %copy-done.5, ...), custom_call_target="tpu_custom_call" | custom-call | flops 42949672960 | bytes 10485760 | tf_op jit(solution)/shard_map/att_bwd/pallas_call | solution.py:515
  459.2 2.1 pad_maximum_fusion.2
  461.3 0.6 pad_maximum_fusion.4.vec_ref
  461.9 56.1 %finish.1 = (f32[512,1024]{1,0:T(8,128)}, f32[1024,256]{1,0:T(8,128)}, f32[1024,256]{1,0:T(8,128)}, f32[1024,256]{1,0:T(8,128)}, f32[8,1024]{1,0:T(8,128)}) custom-call(bf16[2048,1024]{1,0:T(8,128)(2,1)} %all-gather.7.cloned.1.call-done.x_ref, bf16[2048,768]{1,0:T(8,128)(2,1)} %get-tuple-element.53.pk_ref, bf16[4,512,768]{2,1,0:T(8,128)(2,1)} %get-tuple-element.54.own_ref, ...), custom_call_target="tpu_custom_call" | custom-call | flops 6442450944 | bytes 20971520 | tf_op jit(solution)/shard_map/finish/pallas_call | solution.py:707
  518.0 1.5 fusion.28
  519.5 2.8 fusion.7
  522.6 1.1 slice.88
  523.7 4.0 fusion.26
  527.6 1.1 bitcast_convert_fusion.3
  528.8 2.6 bitcast_convert_fusion
  531.4 2.6 bitcast_convert_fusion.1
  534.0 5.3 copy.49
  539.3 2.6 bitcast_convert_fusion.2
  541.9 5.5 copy.48
  547.4 1.3 copy.57
  548.7 0.6 copy-done.25
  549.3 1.0 copy.58
  550.3 0.6 copy-done.24
  550.9 1.0 copy.59
  551.9 1.0 copy.60
  (84 shorter events, 4.3 us)
Async XLA Ops:
  7.2 7.0 %copy-start = (bf16[1024,1024]{1,0:T(8,128)(2,1)S(1)}, bf16[1024,1024]{1,0:T(8,128)(2,1)}, u32[]{:S(2)}) copy-start(bf16[1024,1024]{1,0:T(8,128)(2,1)} %param.26) | copy-start | bytes 6291460
  7.2 3.3 copy-start.18
  7.2 3.3 copy-start.29
  7.2 3.3 copy-start.27
  7.2 84.3 %all-gather.7.cloned.1.call-start = ((), (), s32[]{:S(2)}) async-start(), calls=%async_computation.1 | async-start | bytes 5242880 | tf_op jit(solution)/shard_map/all_gather | solution.py:946
  12.0 170.6 %all-gather.9.cloned.1.call-start = ((), (), s32[]{:S(2)}) async-start(), calls=%async_computation.2 | async-start | bytes 3932160 | tf_op jit(solution)/shard_map/all_gather | solution.py:961
  13.1 3.8 copy-start.6
  14.1 3.0 copy-start.8
  16.2 283.1 %all-gather.11.cloned.1.call-start = ((), (), s32[]{:S(2)}) async-start(), calls=%async_computation.4 | async-start | bytes 7864320 | tf_op jit(solution)/shard_map/all_gather | solution.py:976
  17.3 1.0 copy-start.10
  24.6 78.3 %copy-start.3 = (f32[2048,128]{1,0:T(8,128)}, f32[2048,128]{1,0:T(8,128)S(1)}, u32[]{:S(2)}) copy-start(f32[2048,128]{1,0:T(8,128)S(1)} %get-tuple-element.83.sin_ref) | copy-start | bytes 3145732
  24.6 78.3 %copy-start.4 = (f32[2048,128]{1,0:T(8,128)}, f32[2048,128]{1,0:T(8,128)S(1)}, u32[]{:S(2)}) copy-start(f32[2048,128]{1,0:T(8,128)S(1)} %get-tuple-element.84.cos_ref) | copy-start | bytes 3145732
  91.5 1.0 copy-start.7
  92.6 1.0 copy-start.9
  93.6 1.0 copy-start.11
  94.7 2.2 copy-start.12
  102.9 72.4 %copy-start.13 = (bf16[4,2048,128]{2,1,0:T(8,128)(2,1)}, bf16[4,2048,128]{2,1,0:T(8,128)(2,1)S(1)}, u32[]{:S(2)}) copy-start(bf16[4,2048,128]{2,1,0:T(8,128)(2,1)S(1)} %get-tuple-element.39.q_ref) | copy-start | bytes 6291460
  102.9 72.4 %copy-start.14 = (bf16[4,2048,128]{2,1,0:T(8,128)(2,1)}, bf16[4,2048,128]{2,1,0:T(8,128)(2,1)S(1)}, u32[]{:S(2)}) copy-start(bf16[4,2048,128]{2,1,0:T(8,128)(2,1)S(1)} %get-tuple-element.40.k_ref) | copy-start | bytes 6291460
  102.9 72.4 %copy-start.15 = (bf16[4,2048,128]{2,1,0:T(8,128)(2,1)}, bf16[4,2048,128]{2,1,0:T(8,128)(2,1)S(1)}, u32[]{:S(2)}) copy-start(bf16[4,2048,128]{2,1,0:T(8,128)(2,1)S(1)} %get-tuple-element.41.v_ref) | copy-start | bytes 6291460
  175.3 1.0 copy-start.17
  176.2 1.3 copy-start.2
  176.2 1.7 copy-start.16
  176.2 3.0 copy-start.5
  178.3 1.2 copy-start.19
  180.4 0.7 copy-start.26
  180.4 0.7 copy-start.28
  182.5 276.7 %reduce-scatter.2.cloned.1.call-start = ((), (), s32[]{:S(2)}) async-start(), calls=%async_computation.3 | async-start | bytes 3932160 | tf_op jit(solution)/shard_map/reduce_scatter | solution.py:985
  288.7 233.9 %all-gather.13.cloned.1.call-start = ((), (), s32[]{:S(2)}) async-start(), calls=%async_computation.5 | async-start | bytes 7667712 | tf_op jit(solution)/shard_map/all_gather | solution.py:991
  291.8 1.2 copy-start.20
  461.9 57.6 %copy-start.21 = (bf16[3,512,1024]{2,1,0:T(8,128)(2,1)S(1)}, bf16[3,512,1024]{2,1,0:T(8,128)(2,1)}, u32[]{:S(2)}) copy-start(bf16[3,512,1024]{2,1,0:T(8,128)(2,1)} %get-tuple-element.52) | copy-start | bytes 9437188
  541.9 5.5 copy-start.22
  547.4 2.0 copy-start.25
  549.3 1.6 copy-start.24
  549.3 2.6 copy-start.23
  549.3 3.5 copy-start.1
Sparse Core Ops, SparseCore 0:
  12.1 79.3 all-gather.6
  93.7 88.5 all-gather.8
  183.8 115.3 all-gather.10
  301.4 132.5 reduce-scatter.1
  461.4 61.1 all-gather.12

commit v3 on v2

--- a/solution.py
+++ b/solution.py
@@ -39,69 +39,20 @@
     return jnp.where(first, pltpu.roll(x, width - HD // 2, 1), pltpu.roll(x, HD // 2, 1))
 
 
+STEP = 64
+
+
 def angle_tables(length):
     half = HD // 2
     lane = lax.optimization_barrier(lax.iota(jnp.int32, 2 * HD))
     freqs = 10000.0 ** (-((lane % half).astype(F32) * 2.0 / HD))
-    angles = lax.iota(F32, length)[:, None] * freqs[None, :]
     sign = jnp.where(lane % HD < half, -1.0, 1.0)
-    return jnp.cos(angles), jnp.sin(angles) * sign[None, :]
-
-
-def project_kernel(
-    limit_ref, x_ref, wq_ref, wk_ref, wv_ref, cos_ref, sin_ref, q_ref, k_ref, v_ref
-):
-    x = x_ref[...]
-    block = x.shape[0]
-    heads = q_ref.shape[0]
-    width = heads * HD
-    cosine = jnp.tile(cos_ref[...], (1, heads // 2))
-    sine = jnp.tile(sin_ref[...], (1, heads // 2))
-    lane = lanes((block, 128))
-    row = pl.program_id(0) * block + lax.broadcasted_iota(jnp.int32, (block, 128), 0)
-    ones = jnp.where(lane < HD + 3, 1.0, 0.0)
-    bias = jnp.where(lane == HD + 3, jnp.where(row < limit_ref[0], 0.0, -1e30), ones)
-    unit = jnp.where(lane == HD + 3, 1.0, 0.0)
-
-    def turned(w_ref):
-        raw = dot(x, w_ref[...])
-        return raw * cosine + partner(raw) * sine
-
-    def put(out_ref, values, extra):
-        for h in range(heads):
-            own = values[:, h // 2 * 128 : h // 2 * 128 + 128]
-            own = pltpu.roll(own, HD, 1) if h % 2 else own
-            out_ref[h] = jnp.where(lane < HD, own, extra).astype(BF)
-
-    put(q_ref, turned(wq_ref).astype(BF).astype(F32) * SCALE, unit)
-    put(k_ref, turned(wk_ref), bias)
-    put(v_ref, dot(x, wv_ref[...]), ones)
-
-
-def project(rows, w_query, w_key, w_value, cosine, sine, limit, block=512):
-    n, depth = rows.shape
-    width = w_query.shape[1]
-    heads = width // HD
-    whole = pl.BlockSpec((depth, width), lambda i, *_: (0, 0))
-    table = pl.BlockSpec((block, 2 * HD), lambda i, *_: (i, 0))
-    out = pl.BlockSpec((heads, block, 128), lambda i, *_: (0, i, 0))
-    return pl.pallas_call(
-        project_kernel,
-        out_shape=(jax.ShapeDtypeStruct((heads, n, 128), BF),) * 3,
-        grid_spec=pltpu.PrefetchScalarGridSpec(
-            num_scalar_prefetch=1,
-            grid=(n // block,),
-            in_specs=[pl.BlockSpec((block, depth), lambda i, *_: (i, 0))]
-            + [whole] * 3
-            + [table] * 2,
-            out_specs=(out, out, out),
-        ),
-        compiler_params=pltpu.CompilerParams(vmem_limit_bytes=40 << 20),
-        cost_estimate=pl.CostEstimate(
-            flops=2 * n * depth * 3 * width, bytes_accessed=2 * (n * depth + 6 * n * width), transcendentals=0
-        ),
-        name="project",
-    )(limit, rows, w_query, w_key, w_value, cosine, sine)
+
+    def table(positions):
+        angles = positions[:, None] * freqs[None, :]
+        return jnp.stack([jnp.cos(angles), jnp.sin(angles)])
+
+    return table(lax.iota(F32, length // STEP) * STEP), table(lax.iota(F32, STEP)), sign[None, :]
 
 
 def differ(a, b, bits):
@@ -141,10 +92,221 @@
     pl.semaphore_wait(barrier, n + chips - 2 + both_cores)
 
 
+def begin_kernel(
+    n, chips, chunks, limit_ref, tokens_ref, ct_ref, gain_ref, shift_ref, wq_ref, wk_ref, wv_ref,
+    coarse_ref, fine_ref, sign_ref,
+    q_ref, k_ref, v_ref, cos_ref, sin_ref, rows_ref, gb_all, landed, gb,
+    right_send, right_recv, left_send, left_recv, gs_send, gs_recv, gr_send, gr_recv, keep_sem, rows_sem,
+):
+    me = lax.axis_index("tensor")
+    place = lax.axis_index("dp")
+    core = lax.rem(place, 2)
+    bits = chips.bit_length() - 1
+    rows, depth = tokens_ref.shape
+    heads = q_ref.shape[0]
+    piece = rows // chunks
+    limit = limit_ref[0]
+
+    def over(shard, d, c, send, recv, to):
+        part = landed.at[shard, pl.ds(c * piece, piece)]
+        return remote(part, part, send.at[d, c], recv.at[d, c], tensor=to)
+
+    def rightward(d, c):
+        return over(me - d, d, c, right_send, right_recv, me + 1)
+
+    def leftward(d, c):
+        return over(me + d, d, c, left_send, left_recv, me - 1)
+
+    def from_left(d, c):
+        return over(me - d, d - 1, c, right_send, right_recv, me - 1)
+
+    def from_right(d, c):
+        return over(me + d, d - 1, c, left_send, left_recv, me + 1)
+
+    def spread_gb(c):
+        return remote(
+            gb, gb_all.at[place // 2, core], gs_send.at[c], gs_recv.at[c], dp=same_core(c, chips)
+        )
+
+    def relay_gb(c):
+        there = gb_all.at[differ(place // 2, c, bits), core]
+        return remote(there if c else gb, there, gr_send.at[c], gr_recv.at[c], dp=sibling())
+
+    barrier = pltpu.get_barrier_semaphore()
+    pl.semaphore_signal(barrier, inc=1, device_id={"dp": sibling()}, device_id_type=MESH)
+    for s in range(1, chips):
+        to = same_core(s, chips)
+        pl.semaphore_signal(barrier, inc=1, device_id={"dp": to}, device_id_type=MESH)
+
+    @pl.when(me > 0)
+    def _():
+        pl.semaphore_signal(barrier, inc=1, device_id={"tensor": me - 1}, device_id_type=MESH)
+
+    @pl.when(me < n - 1)
+    def _():
+        pl.semaphore_signal(barrier, inc=1, device_id={"tensor": me + 1}, device_id_type=MESH)
+
+    values = tokens_ref[...].astype(F32)
+    values = values - jnp.mean(values, axis=1, keepdims=True)
+    inverse = lax.rsqrt(jnp.mean(values * values, axis=1, keepdims=True) + EPS)
+    landed[me] = (values * inverse * gain_ref[...] + shift_ref[...]).astype(BF)
+
+    pl.semaphore_wait(barrier, chips + jnp.minimum(me, 1) + jnp.minimum(n - 1 - me, 1))
+
+    for c in range(chunks):
+
+        @pl.when(me < n - 1)
+        def _():
+            rightward(0, c).start()
+
+        @pl.when(me > 0)
+        def _():
+            leftward(0, c).start()
+
+    row = me * rows + lax.broadcasted_iota(jnp.int32, (rows, depth), 0)
+    gb[...] = jnp.where(row < limit, ct_ref[...].astype(F32), 0.0).astype(BF)
+    for s in range(1, chips):
+        spread_gb(s).start()
+    relay_gb(0).start()
+    keep = pltpu.make_async_copy(gb, gb_all.at[place // 2, core], keep_sem)
+    keep.start()
+
+    lane = lanes((rows, 128))
+    ones = jnp.where(lane < HD + 3, 1.0, 0.0)
+    unit = jnp.where(lane == HD + 3, 1.0, 0.0)
+
+    def put(out_ref, here, values, extra):
+        for h in range(heads):
+            own = values[:, h // 2 * 128 : h // 2 * 128 + 128]
+            own = pltpu.roll(own, HD, 1) if h % 2 else own
+            out_ref[h, here, :] = jnp.where(lane < HD, own, extra).astype(BF)
+
+    def project(shard):
+        here = pl.ds(pl.multiple_of(shard * rows, rows), rows)
+        for i in range(rows // STEP):
+            part = pl.ds(pl.multiple_of(shard * rows + i * STEP, STEP), STEP)
+            coarse = pl.ds(shard * (rows // STEP) + i, 1)
+            c0, s0 = coarse_ref[0, coarse, :], coarse_ref[1, coarse, :]
+            cos_ref[part, :] = c0 * fine_ref[0] - s0 * fine_ref[1]
+            sin_ref[part, :] = (s0 * fine_ref[0] + c0 * fine_ref[1]) * sign_ref[...]
+        cosine = jnp.tile(cos_ref[here, :], (1, heads // 2))
+        sine = jnp.tile(sin_ref[here, :], (1, heads // 2))
+        x = landed[shard]
+        row = shard * rows + lax.broadcasted_iota(jnp.int32, (rows, 128), 0)
+        bias = jnp.where(lane == HD + 3, jnp.where(row < limit, 0.0, -1e30), ones)
+        raw = dot(x, wq_ref[...])
+        turned = (raw * cosine + partner(raw) * sine).astype(BF).astype(F32)
+        put(q_ref, here, turned * SCALE, unit)
+        raw = dot(x, wk_ref[...])
+        put(k_ref, here, raw * cosine + partner(raw) * sine, bias)
+        put(v_ref, here, dot(x, wv_ref[...]), ones)
+
+    def save(shard):
+        return pltpu.make_async_copy(landed.at[shard], rows_ref.at[shard], rows_sem.at[shard])
+
+    for d in range(1, n + 1):
+        for c in range(chunks):
+            if d < n:
+
+                @pl.when(me >= d)
+                def _():
+                    from_left(d, c).wait_recv()
+
+                @pl.when((me >= d) & (me < n - 1))
+                def _():
+                    rightward(d, c).start()
+
+                @pl.when(me + d < n)
+                def _():
+                    from_right(d, c).wait_recv()
+
+                @pl.when((me + d < n) & (me > 0))
+                def _():
+                    leftward(d, c).start()
+
+            if c == 0:
+
+                @pl.when(me >= d - 1)
+                def _():
+                    save(me - d + 1).start()
+                    project(me - d + 1)
+
+            if c == 1 and d > 1:
+
+                @pl.when(me + d - 1 < n)
+                def _():
+                    save(me + d - 1).start()
+                    project(me + d - 1)
+
+            if c == chunks - 1 and d == 2:
+                for s in range(1, chips // 2 + 1):
+                    spread_gb(s).wait_recv()
+                    relay_gb(s).start()
+
+            if c == 0 and d == n:
+                for s in range(chips // 2 + 1, chips):
+                    spread_gb(s).wait_recv()
+                    relay_gb(s).start()
+
+    for d in range(n - 1):
+        for c in range(chunks):
+
+            @pl.when((me >= d) & (me < n - 1))
+            def _():
+                rightward(d, c).wait_send()
+
+            @pl.when((me + d < n) & (me > 0))
+            def _():
+                leftward(d, c).wait_send()
+
+    for s in range(chips):
+        relay_gb(s).wait()
+        if s:
+            spread_gb(s).wait_send()
+    keep.wait()
+    for shard in range(n):
+        save(shard).wait()
+
+
+def begin(tokens, cotangent, gain, shift, w_query, w_key, w_value, tables, limit, n, devices):
+    rows, depth = tokens.shape
+    total = n * rows
+    heads = w_query.shape[1] // HD
+    chips = devices // 2
+    chunks = 4
+    vmem = pl.BlockSpec(memory_space=pltpu.VMEM)
+    hbm = pl.BlockSpec(memory_space=pl.ANY)
+    return pl.pallas_call(
+        functools.partial(begin_kernel, n, chips, chunks),
+        out_shape=(jax.ShapeDtypeStruct((heads, total, 128), BF),) * 3
+        + (jax.ShapeDtypeStruct((total, 128), F32),) * 2
+        + (
+            jax.ShapeDtypeStruct((n, rows, depth), BF),
+            jax.ShapeDtypeStruct((chips, 2, rows, depth), BF),
+        ),
+        in_specs=[pl.BlockSpec(memory_space=pltpu.SMEM)] + [vmem] * 10,
+        out_specs=[vmem] * 5 + [hbm] * 2,
+        scratch_shapes=[pltpu.VMEM((n, rows, depth), BF), pltpu.VMEM((rows, depth), BF)]
+        + [pltpu.SemaphoreType.DMA((n - 1, chunks))] * 4
+        + [pltpu.SemaphoreType.DMA((chips,))] * 4
+        + [pltpu.SemaphoreType.DMA, pltpu.SemaphoreType.DMA((n,))],
+        compiler_params=pltpu.CompilerParams(
+            vmem_limit_bytes=44 << 20, collective_id=5, has_side_effects=True
+        ),
+        cost_estimate=pl.CostEstimate(
+            flops=6 * total * depth * heads * HD * 10, bytes_accessed=30 << 20, transcendentals=0
+        ),
+        name="begin",
+    )(
+        limit, tokens, cotangent, gain.reshape(1, depth), shift.reshape(1, depth),
+        w_query, w_key, w_value, *tables,
+    )
+
+
 def att_fwd_kernel(
-    n, chips, q_ref, k_ref, v_ref, gb_ref, wo_ref,
-    ctx_ref, lse_ref, out_ref, gb_all, wo_z, wo_all, send_sem, recv_sem, own_sem,
-    gs_send, gs_recv, gr_send, gr_recv, wz_send, wz_recv, ws_send, ws_recv, wr_send, wr_recv, keep_sem,
+    n, chips, q_ref, k_ref, v_ref, wo_ref,
+    ctx_ref, lse_ref, out_ref, wo_z, wo_all, send_sem, recv_sem, own_sem,
+    wz_send, wz_recv, ws_send, ws_recv, wr_send, wr_recv, keep_sem,
 ):
     s = pl.program_id(0)
     h = pl.program_id(1)
@@ -155,17 +317,6 @@
     core = lax.rem(place, 2)
     bits = chips.bit_length() - 1
 
-    def spread_gb(c):
-        return remote(
-            gb_ref, gb_all.at[place // 2, core], gs_send.at[c], gs_recv.at[c], dp=same_core(c, chips)
-        )
-
-    def relay_gb(c):
-        there = gb_all.at[differ(place // 2, c, bits), core]
-        return remote(
-            there if c else gb_ref, there, gr_send.at[c], gr_recv.at[c], dp=sibling()
-        )
-
     def wo_over(step):
         return remote(
             wo_ref, wo_z.at[me], wz_send.at[step], wz_recv.at[step], tensor=ring(n, step + 1)
@@ -181,9 +332,8 @@
         return remote(there if c else wo_z, there, wr_send.at[c], wr_recv.at[c], dp=sibling())
 
     keeps = [
-        pltpu.make_async_copy(gb_ref, gb_all.at[place // 2, core], keep_sem.at[0]),
-        pltpu.make_async_copy(wo_ref, wo_z.at[me], keep_sem.at[1]),
-        pltpu.make_async_copy(wo_z, wo_all.at[:, place], keep_sem.at[2]),
+        pltpu.make_async_copy(wo_ref, wo_z.at[me], keep_sem.at[0]),
+        pltpu.make_async_copy(wo_z, wo_all.at[:, place], keep_sem.at[1]),
     ]
 
     @pl.when((s == 0) & (h == 0))
@@ -192,35 +342,22 @@
         for step in range(n - 1):
             wo_over(step).start()
         keeps[0].start()
-        keeps[1].start()
-        for c in range(1, chips):
-            spread_gb(c).start()
-        relay_gb(0).start()
 
     @pl.when((s == 1) & (h == 0))
     def _():
         for step in range(n - 1):
             wo_over(step).wait()
-        keeps[1].wait()
+        keeps[0].wait()
         for c in range(1, chips):
             spread_wo(c).start()
         relay_wo(0).start()
-        keeps[2].start()
-
-    @pl.when((s == n - 2) & (h == 0))
-    def _():
-        for c in range(1, chips // 2 + 1):
-            spread_gb(c).wait_recv()
-            relay_gb(c).start()
+        keeps[1].start()
 
     @pl.when((s == n - 1) & (h == 0))
     def _():
         for c in range(1, chips):
             spread_wo(c).wait_recv()
             relay_wo(c).start()
-        for c in range(chips // 2 + 1, chips):
-            spread_gb(c).wait_recv()
-            relay_gb(c).start()
 
     owner = ring(n, s + 1)
     block = pl.ds(pl.multiple_of(owner * rows, rows), rows)
@@ -257,22 +394,18 @@
         for step in range(n - 1):
             push(step).wait()
         keep.wait()
-        keeps[0].wait()
-        keeps[2].wait()
+        keeps[1].wait()
         for c in range(chips):
-            relay_gb(c).wait()
             relay_wo(c).wait()
             if c:
-                spread_gb(c).wait_send()
                 spread_wo(c).wait_send()
 
 
-def att_fwd(q, k, v, grad_rows, w_out_piece, n, devices):
+def att_fwd(q, k, v, w_out_piece, n, devices):
     heads, total, _ = q.shape
     width = heads * HD
     rows = total // n
-    depth = grad_rows.shape[1]
-    share = w_out_piece.shape[0]
+    share, depth = w_out_piece.shape
     chips = devices // 2
     hbm = pl.BlockSpec(memory_space=pl.ANY)
 
@@ -285,21 +418,19 @@
             jax.ShapeDtypeStruct((total, width), BF),
             jax.ShapeDtypeStruct((total, 128), F32),
             jax.ShapeDtypeStruct((n, rows, width), BF),
-            jax.ShapeDtypeStruct((chips, 2, rows, depth), BF),
             jax.ShapeDtypeStruct((n, share, depth), BF),
             jax.ShapeDtypeStruct((n, devices, share, depth), BF),
         ),
         grid_spec=pltpu.PrefetchScalarGridSpec(
             num_scalar_prefetch=0,
             grid=(n, heads),
-            in_specs=[whole(heads, total, 128)] * 3 + [hbm] * 2,
-            out_specs=[whole(total, width), whole(total, 128)] + [hbm] * 4,
+            in_specs=[whole(heads, total, 128)] * 3 + [hbm],
+            out_specs=[whole(total, width), whole(total, 128)] + [hbm] * 3,
             scratch_shapes=[pltpu.SemaphoreType.DMA((n - 1,))] * 2
             + [pltpu.SemaphoreType.DMA]
-            + [pltpu.SemaphoreType.DMA((chips,))] * 4
             + [pltpu.SemaphoreType.DMA((n - 1,))] * 2
             + [pltpu.SemaphoreType.DMA((chips,))] * 4
-            + [pltpu.SemaphoreType.DMA((3,))],
+            + [pltpu.SemaphoreType.DMA((2,))],
         ),
         compiler_params=pltpu.CompilerParams(
             vmem_limit_bytes=40 << 20, collective_id=1, has_side_effects=True
@@ -310,7 +441,7 @@
             transcendentals=total * total * heads,
         ),
         name="att_fwd",
-    )(q, k, v, grad_rows, w_out_piece)
+    )(q, k, v, w_out_piece)
 
 
 def att_bwd_kernel(
@@ -907,6 +1038,42 @@
     )(x, grad_branch, weights)
 
 
+def unpack_kernel(share, g_ref, gate_ref, up_ref, down_ref, out_ref):
+    g = g_ref[0].astype(F32)
+    gate_ref[...] = g[:share].T
+    up_ref[...] = g[share : 2 * share].T
+    down_ref[...] = g[2 * share : 3 * share]
+    out_ref[...] = g[3 * share :]
+
+
+def unpack(grads, share, width):
+    devices, height, depth = grads.shape
+    hidden = devices * share
+    if share % 128:
+        gate, up, down = (
+            grads[:, k * share : (k + 1) * share].reshape(hidden, depth).astype(F32) for k in range(3)
+        )
+        return gate.T, up.T, down, grads[:, 3 * share :].reshape(width, depth).astype(F32)
+    column = pl.BlockSpec((depth, share), lambda i: (0, i))
+    return pl.pallas_call(
+        functools.partial(unpack_kernel, share),
+        out_shape=(
+            jax.ShapeDtypeStruct((depth, hidden), F32),
+            jax.ShapeDtypeStruct((depth, hidden), F32),
+            jax.ShapeDtypeStruct((hidden, depth), F32),
+            jax.ShapeDtypeStruct((width, depth), F32),
+        ),
+        grid=(devices,),
+        in_specs=[pl.BlockSpec((1, height, depth), lambda i: (i, 0, 0))],
+        out_specs=[
+            column, column, pl.BlockSpec((share, depth), lambda i: (i, 0)),
+            pl.BlockSpec((width // devices, depth), lambda i: (i, 0)),
+        ],
+        compiler_params=pltpu.CompilerParams(vmem_limit_bytes=40 << 20),
+        name="unpack",
+    )(grads)
+
+
 def norm_parts(values):
     centre = jnp.mean(values, axis=-1, keepdims=True)
     centred = values - centre
@@ -942,13 +1109,7 @@
     row_ids = lax.axis_index("tensor") * local_rows + lax.iota(jnp.int32, local_rows)
     valid = (row_ids < lengths[0])[:, None]
 
-    def gather(x):
-        return lax.all_gather(x, "tensor", axis=0, tiled=True)
-
     inputs = tokens.astype(F32)
-    scaled1, _ = norm_parts(inputs)
-    attn_rows = gather((scaled1 * ln1_gain + ln1_bias).astype(BF))
-    cosine, sine = angle_tables(length)
     grad_out = jnp.where(valid, cotangent.astype(F32), 0.0)
     devices = lax.axis_size("dp")
     place = lax.axis_index("dp")
@@ -958,10 +1119,15 @@
         return lax.dynamic_slice_in_dim(x, place * share, share, axis)
 
     weights = jnp.stack([piece(w_gate, 1).T, piece(w_up, 1).T, piece(down_weight, 0)])
+    q, k, v, cosine, sine, attn_rows, grad_branch = begin(
+        tokens, cotangent, ln1_gain, ln1_bias, w_query, w_key, w_value, angle_tables(length),
+        lengths, n, devices,
+    )
+    attn_rows = attn_rows.reshape(length, depth)
+    weights, q = lax.optimization_barrier((weights, q))
     weights = lax.all_gather(weights, "tensor", axis=1, tiled=True)
-    q, k, v = project(attn_rows, w_query, w_key, w_value, cosine, sine, lengths)
-    context, logsum, context_own, grad_branch, _, w_out_all = att_fwd(
-        q, k, v, grad_out.astype(BF),
+    context, logsum, context_own, _, w_out_all = att_fwd(
+        q, k, v,
         lax.dynamic_slice_in_dim(w_out, place * (width // devices), width // devices, 0),
         n, devices,
     )
@@ -989,12 +1155,7 @@
     )
     ffn_grads, out_piece = lax.optimization_barrier((ffn_grads, out_piece))
     grads = lax.all_gather(jnp.concatenate([ffn_grads, out_piece]), "dp", axis=0)
-    gate_grad, up_grad, down_grad = (
-        grads[:, k * share : (k + 1) * share].reshape(devices * share, depth).astype(F32)
-        for k in range(3)
-    )
-    gate_grad, up_grad = gate_grad.T, up_grad.T
-    out_grad = grads[:, 3 * share :].reshape(width, depth).astype(F32)
+    gate_grad, up_grad, down_grad, out_grad = unpack(grads, share, width)
     ffn_out = sum(x.astype(F32) for x in (out_parts[0], *out_sums))
     output = jnp.where(valid, middle + ffn_out, 0.0).astype(BF)
     input_grad, query_grad, key_grad, value_grad, sums = finish(

time: 567 us -> 559 us (0.986)
  Pallas kernels: 400 us -> 470 us
  waiting for transfers between devices: 68.9 us -> 4.94 us
  other arithmetic: 36.7 us -> 20.8 us
    pallas_call x1 -> x2, Pallas kernels: 5.99 us -> 76.7 us  [the longest x1 70.9 us: begin(): pl.pallas_call(functools.partial(begin_kernel, n, chips, chunks), out_sha...]
    all_gather x1 -> x0, waiting for transfers between devices: 64.7 us -> none  [gather(): return lax.all_gather(x, 'tensor', axis=0, tiled=True)]
    unnamed x69 -> x75, local copies, waits for them, and re-layouts: 16.6 us -> 29.1 us
    transpose x2 -> x0, local copies, waits for them, and re-layouts: 10.8 us -> none  [on_device(): gate_grad, up_grad = (gate_grad.T, up_grad.T)]
    convert_element_type x4 -> x0, other arithmetic: 7.37 us -> none  [the longest x1 2.61 us: on_device(): grads[:, k * share:(k + 1) * share].reshape(devices * share, depth)]
    pallas_call x1, Pallas kernels: 106 us -> 100 us  [ffn(): pl.pallas_call(functools.partial(ffn_kernel, chips), out_shape=(jax.Shape...]
  transfers between devices with their start and end apart: 5 -> 4, of which waited for: 3 -> 2; matrix products, arithmetic and copies ran while one was open for 5% -> 4% of each run, Pallas kernels for 72% -> 72%
where the time goes in v3:
time: 559 us; the launch traced here: 548 us
  Pallas kernels  470 us (84%)
  local copies, waits for them, and re-layouts  33.9 us (6%)
  other arithmetic  20.8 us (4%)
  between operations  15.2 us (3%)
    pallas_call x1, Pallas kernels, att_bwd(): pl.pallas_call(functools.partial(att_bwd_kernel, n, bk, chips), out_shape...  160 us
    pallas_call x1, Pallas kernels, ffn(): pl.pallas_call(functools.partial(ffn_kernel, chips), out_shape=(jax.Shape...  100 us
    pallas_call x1, Pallas kernels, att_fwd(): pl.pallas_call(functools.partial(att_fwd_kernel, n, chips), out_shape=(ja...  77.8 us
    pallas_call x1, Pallas kernels, begin(): pl.pallas_call(functools.partial(begin_kernel, n, chips, chunks), out_sha...  70.9 us
    pallas_call x1, Pallas kernels, finish(): pl.pallas_call(functools.partial(finish_kernel, chips, n, width), out_sha...  55.6 us
    unnamed x75, local copies, waits for them, and re-layouts  29.1 us
  transfers between devices with their start and end apart: 4, of which 2 were waited for; matrix products, arithmetic and copies ran while one was open for 4% of the time, Pallas kernels for 72%

profile of v3, /device:TPU:9, one launch (start us, length us, event | category | flops | bytes accessed | tf_op | source)
XLA Modules:
  0.0 548.4 jit_solution(12090066383243783473)
XLA Ops:
  8.1 0.8 fusion.13
  9.1 2.0 constant_dynamic-slice_fusion.1
  11.1 1.8 copy.43
  12.9 1.8 copy.42
  14.7 0.8 pad_maximum_fusion.4.fine_ref
  15.5 2.0 pad_maximum_fusion.3
  17.5 1.0 copy-done.10
  18.6 70.9 %begin.1 = (bf16[4,2048,128]{2,1,0:T(8,128)(2,1)S(1)}, bf16[4,2048,128]{2,1,0:T(8,128)(2,1)S(1)}, bf16[4,2048,128]{2,1,0:T(8,128)(2,1)}, f32[2048,128]{1,0:T(8,1...) custom-call(s32[1]{0:T(128)} %copy.48.limit_ref, ...), custom_call_target="tpu_custom_call" | custom-call | flops 32212254720 | bytes 31457280 | tf_op jit(solution)/shard_map/begin/pallas_call | solution.py:279
  89.5 1.3 copy-done.14
  90.8 1.3 copy-done.16
  92.1 1.0 copy-done.21
  93.1 1.0 copy-done.22
  94.4 1.0 copy.38
  95.4 1.0 copy.39
  96.4 1.0 copy.41
  97.4 1.1 pad_maximum_fusion.1
  98.6 0.9 constant_dynamic-slice_fusion.wo_ref
  99.5 2.3 pad_maximum_fusion
  101.8 1.6 copy-done.15
  103.4 1.6 copy-done.17
  105.0 1.6 copy-done.18
  106.5 77.8 %att_fwd.1 = (bf16[2048,256]{1,0:T(8,128)(2,1)S(1)}, f32[2048,128]{1,0:T(8,128)S(1)}, bf16[4,512,256]{2,1,0:T(8,128)(2,1)S(1)}, bf16[4,32,1024]{2,1,0:T(8,128)(2,1)}, bf16[4,8,32,1024]{3,2,1,0:T(8,128)(2,1)S(1)}) custom-call(bf16[4,2048,128]{2,1,0:T(8,128)(2,1)S(1)} %copy-done.15, bf16[4,2048,128]{2,1,0:T(8,128)(2,1)S(1)} %copy-done.17, ...), custom_call_target="tpu_custom_call" | custom-call | flops 17179869184 | bytes 5242880 | tf_op jit(solution)/shard_map/att_fwd/pallas_call | solution.py:415
  184.3 1.0 copy-done.20
  185.5 1.1 copy-done.3
  187.4 0.4 convolution_convert_fusion.2
  188.6 0.8 fusion.23
  189.9 0.9 copy-done.23
  190.8 1.4 add_convert_fusion.x_ref
  192.2 0.4 reduce-scatter.2.cloned.1.call-start
  192.7 100.2 %ffn.1 = (bf16[4,512,1024]{2,1,0:T(8,128)(2,1)}, bf16[4,512,1024]{2,1,0:T(8,128)(2,1)}, bf16[4,3,128,1024]{3,2,1,0:T(8,128)(2,1)}) custom-call(bf16[512,1024]{1,0:T(8,128)(2,1)} %add_convert_fusion.x_ref, bf16[4,2,512,1024]{3,2,1,0:T(8,128)(2,1)} %get-tuple-element.55.gb_ref, bf16[3,512,1024]{2,1,0:T(8,128)(2,1)} %all-gather.6.cloned.1.call-done.w_ref), custom_call_target="tpu_custom_call" | custom-call | flops 38654705664 | bytes 31457280 | tf_op jit(solution)/shard_map/ffn/pallas_call | solution.py:1009
  293.1 3.2 fusion.19
  296.4 1.0 fusion.2
  297.4 2.2 fusion.20
  299.5 4.6 all-gather.8.cloned.1.call-done
  304.2 160.2 %att_bwd.1 = (bf16[2048,768]{1,0:T(8,128)(2,1)}, bf16[4,512,768]{2,1,0:T(8,128)(2,1)}, bf16[3,512,1024]{2,1,0:T(8,128)(2,1)}, bf16[32,1024]{1,0:T(8,128)(2,1)}) custom-call(bf16[512,1024]{1,0:T(8,128)(2,1)} %get-tuple-element.60.ga_ref, bf16[4,256,1024]{2,1,0:T(8,128)(2,1)} %bitcast.75, bf16[4,512,256]{2,1,0:T(8,128)(2,1)} %copy-done.7, ...), custom_call_target="tpu_custom_call" | custom-call | flops 42949672960 | bytes 10485760 | tf_op jit(solution)/shard_map/att_bwd/pallas_call | solution.py:646
  464.5 2.1 pad_maximum_fusion.2
  466.6 0.6 pad_maximum_fusion.6.vec_ref
  467.2 55.6 %finish.1 = (f32[512,1024]{1,0:T(8,128)}, f32[1024,256]{1,0:T(8,128)}, f32[1024,256]{1,0:T(8,128)}, f32[1024,256]{1,0:T(8,128)}, f32[8,1024]{1,0:T(8,128)}) custom-call(bf16[2048,1024]{1,0:T(8,128)(2,1)} %bitcast.98, bf16[2048,768]{1,0:T(8,128)(2,1)} %get-tuple-element.67.pk_ref, bf16[4,512,768]{2,1,0:T(8,128)(2,1)} %get-tuple-element.68.own_ref, ...), custom_call_target="tpu_custom_call" | custom-call | flops 6442450944 | bytes 20971520 | tf_op jit(solution)/shard_map/finish/pallas_call | solution.py:838
  522.9 1.5 fusion.22
  524.4 2.8 fusion.1
  527.5 2.9 copy-done.2
  530.4 5.7 %unpack.1 = (f32[1024,1024]{1,0:T(8,128)}, f32[1024,1024]{1,0:T(8,128)}, f32[1024,1024]{1,0:T(8,128)}, f32[256,1024]{1,0:T(8,128)}) custom-call(bf16[8,416,1024]{2,1,0:T(8,128)(2,1)S(1)} %bitcast.74), custom_call_target="tpu_custom_call" | custom-call | tf_op jit(solution)/shard_map/unpack/pallas_call | solution.py:1058
  536.1 1.3 copy.49
  537.4 0.6 copy-done.30
  538.1 1.0 copy.50
  539.1 0.6 copy-done.29
  539.7 1.0 copy.51
  540.7 1.0 copy.52
  (78 shorter events, 3.3 us)
Async XLA Ops:
  7.2 1.8 copy-start
  7.2 185.5 %all-gather.6.cloned.1.call-start = ((), (), s32[]{:S(2)}) async-start(), calls=%async_computation.1 | async-start | bytes 3932160 | tf_op jit(solution)/shard_map/all_gather | solution.py:1128
  9.0 8.5 %copy-start.4 = (bf16[512,1024]{1,0:T(8,128)(2,1)S(1)}, bf16[512,1024]{1,0:T(8,128)(2,1)}, u32[]{:S(2)}) copy-start(bf16[512,1024]{1,0:T(8,128)(2,1)} %ct_ref.1) | copy-start | bytes 3145732
  9.0 8.5 %copy-start.12 = (f32[1024]{0:T(1024)S(1)}, f32[1024]{0:T(1024)}, u32[]{:S(2)}) copy-start(f32[1024]{0:T(1024)} %param.17) | copy-start | bytes 12292
  9.0 8.5 %copy-start.13 = (f32[1024]{0:T(1024)S(1)}, f32[1024]{0:T(1024)}, u32[]{:S(2)}) copy-start(f32[1024]{0:T(1024)} %param.16) | copy-start | bytes 12292
  9.1 8.4 %copy-start.5 = (bf16[512,1024]{1,0:T(8,128)(2,1)S(1)}, bf16[512,1024]{1,0:T(8,128)(2,1)}, u32[]{:S(2)}) copy-start(bf16[512,1024]{1,0:T(8,128)(2,1)} %tokens_ref.3) | copy-start | bytes 3145732
  9.1 8.4 %copy-start.8 = (bf16[1024,256]{1,0:T(8,128)(2,1)S(1)}, bf16[1024,256]{1,0:T(8,128)(2,1)}, u32[]{:S(2)}) copy-start(bf16[1024,256]{1,0:T(8,128)(2,1)} %wq_ref.1) | copy-start | bytes 1572868
  9.1 8.4 %copy-start.9 = (bf16[1024,256]{1,0:T(8,128)(2,1)S(1)}, bf16[1024,256]{1,0:T(8,128)(2,1)}, u32[]{:S(2)}) copy-start(bf16[1024,256]{1,0:T(8,128)(2,1)} %wk_ref.1) | copy-start | bytes 1572868
  17.5 1.0 copy-start.10
  89.5 1.3 copy-start.14
  90.8 1.3 copy-start.16
  92.1 1.0 copy-start.21
  93.1 1.0 copy-start.22
  94.1 2.3 copy-start.11
  94.1 210.1 %all-gather.8.cloned.1.call-start = ((), (), s32[]{:S(2)}) async-start(), calls=%async_computation.3 | async-start | bytes 7864320 | tf_op jit(solution)/shard_map/all_gather | solution.py:1142
  95.4 2.0 copy-start.27
  101.8 1.6 copy-start.15
  103.4 1.6 copy-start.17
  105.0 1.6 copy-start.18
  184.3 1.0 copy-start.20
  185.3 1.3 copy-start.3
  185.3 1.7 copy-start.19
  185.3 3.0 copy-start.7
  187.4 1.2 copy-start.6
  189.5 1.3 copy-start.23
  189.5 1.3 copy-start.31
  189.5 1.3 copy-start.32
  192.2 272.3 %reduce-scatter.2.cloned.1.call-start = ((), (), s32[]{:S(2)}) async-start(), calls=%async_computation.2 | async-start | bytes 3932160 | tf_op jit(solution)/shard_map/reduce_scatter | solution.py:1151
  292.9 234.5 %all-gather.10.cloned.1.call-start = ((), (), s32[]{:S(2)}) async-start(), calls=%async_computation.4 | async-start | bytes 7667712 | tf_op jit(solution)/shard_map/all_gather | solution.py:1157
  293.1 3.2 copy-start.24
  467.2 57.2 %copy-start.25 = (bf16[3,512,1024]{2,1,0:T(8,128)(2,1)S(1)}, bf16[3,512,1024]{2,1,0:T(8,128)(2,1)}, u32[]{:S(2)}) copy-start(bf16[3,512,1024]{2,1,0:T(8,128)(2,1)} %get-tuple-element.65) | copy-start | bytes 9437188
  527.4 2.9 copy-start.2
  530.4 5.7 %copy-start.26 = (f32[512,1024]{1,0:T(8,128)S(1)}, f32[512,1024]{1,0:T(8,128)}, u32[]{:S(2)}) copy-start(f32[512,1024]{1,0:T(8,128)} %get-tuple-element.122) | copy-start | bytes 6291460
  536.1 2.0 copy-start.30
  538.1 1.6 copy-start.29
  538.1 2.6 copy-start.28
  538.1 3.5 copy-start.1
Sparse Core Ops, SparseCore 0:
  94.2 93.6 all-gather.5
  192.3 111.8 all-gather.7
  306.5 133.9 reduce-scatter.1
  466.7 60.6 all-gather.9
